TPU v7x, 32 devices: a 4x2x2 block of a 4x4x8 slice. The times are simulated.
32 devices in a mesh: dp: 4 (over y, z), ep: 8 (over x, core).
Axes of the slice: x: 4, y: 2, z: 2, core: 2. Of those that a mesh axis runs over, the one named last changes fastest.
The devices are a block of a 4x4x8 slice.
Arguments:
- hidden: bfloat16 [32768, 2048], P(('dp', 'ep')), parts along dimension 0
- w_router: bfloat16 [2048, 64], replicated
- w_gate: bfloat16 [64, 2048, 1408], P('ep')
- w_up: bfloat16 [64, 2048, 1408], P('ep')
- w_down: bfloat16 [64, 1408, 2048], P('ep')
- shared_gate: bfloat16 [2048, 2816], replicated
- shared_up: bfloat16 [2048, 2816], replicated
- shared_down: bfloat16 [2816, 2048], replicated
- top_idx: int32 [32768, 6], P(('dp', 'ep')), parts along dimension 0
- keep_mask: int32 [32768, 6], P(('dp', 'ep')), parts along dimension 0
Outputs:
- output: bfloat16 [32768, 2048], P(('dp', 'ep')), parts along dimension 0
There are 4 independent parts. A program takes and returns all parts, laid end to end along the dimension named above; an argument that names none is the same for every part.
All inputs are finite; a program needn't handle non-finite values.
Results may differ from a plain program's by a relative error of at most 0.00691113.
Values are sent between devices in bfloat16 or wider.
A program may use at most 768 MiB of HBM per device.

v0:
```python
import jax
import jax.numpy as jnp
from jax import lax
from jax.sharding import PartitionSpec as P

ROUTE_SCALE = 16.0


def swiglu(tok_rows, gate_w, up_w, down_w):
    h_gate = jnp.dot(tok_rows, gate_w, preferred_element_type=jnp.float32)
    h_up = jnp.dot(tok_rows, up_w, preferred_element_type=jnp.float32)
    act_rows = (jax.nn.silu(h_gate) * h_up).astype(jnp.bfloat16)
    return jnp.dot(act_rows, down_w, preferred_element_type=jnp.float32)


def expert_bank(tok_rows, gate_w, up_w, down_w):
    h_gate = jnp.einsum("erd,edf->erf", tok_rows, gate_w, preferred_element_type=jnp.float32)
    h_up = jnp.einsum("erd,edf->erf", tok_rows, up_w, preferred_element_type=jnp.float32)
    act_rows = (jax.nn.silu(h_gate) * h_up).astype(jnp.bfloat16)
    return jnp.einsum("erf,efd->erd", act_rows, down_w, preferred_element_type=jnp.float32)


def route_gates(hidden, w_router, top_idx, keep_mask):
    logits = jnp.dot(hidden, w_router, preferred_element_type=jnp.float32)
    router_prob = jax.nn.softmax(logits, axis=-1)
    return ROUTE_SCALE * jnp.take_along_axis(router_prob, top_idx, axis=1) * keep_mask.astype(jnp.float32)


def solution(mesh):
    groups = mesh.shape["ep"]
    tok_spec = P(("dp", "ep"), None)
    bank_spec = P("ep", None, None)

    def device_fn(hidden, w_router, w_gate, w_up, w_down, shared_gate, shared_up, shared_down, top_idx, keep_mask):
        tokens, top_k = top_idx.shape
        hidden_dim = hidden.shape[1]
        experts = w_router.shape[1]
        per_dev = w_gate.shape[0]
        capacity = 8 * ((top_k * tokens + 4 * experts - 1) // (4 * experts))
        n_rows = experts * capacity
        gate_vals = route_gates(hidden, w_router, top_idx, keep_mask)
        pair_expert = top_idx.reshape(-1)
        pair_kept = keep_mask.reshape(-1) > 0
        onehot = ((pair_expert[:, None] == jnp.arange(experts)[None, :]) & pair_kept[:, None]).astype(jnp.int32)
        pair_slot = jnp.sum((jnp.cumsum(onehot, axis=0) - 1) * onehot, axis=1)
        dest_dev = pair_expert // per_dev
        local_exp = pair_expert % per_dev
        dest_row = jnp.where(pair_kept, (local_exp * groups + dest_dev) * capacity + pair_slot, n_rows)
        pair_token = jnp.arange(tokens * top_k, dtype=jnp.int32) // top_k
        row_token = jnp.full((n_rows,), tokens, jnp.int32).at[dest_row].set(pair_token, mode="drop")
        send_rows = jnp.take(hidden, row_token, axis=0, mode="fill", fill_value=0).reshape(per_dev, groups, capacity, hidden_dim)
        recv_rows = lax.all_to_all(send_rows, "ep", 1, 1, tiled=True)
        expert_out = expert_bank(recv_rows.reshape(per_dev, groups * capacity, hidden_dim), w_gate, w_up, w_down).astype(jnp.bfloat16)
        back_rows = lax.all_to_all(expert_out.reshape(per_dev, groups, capacity, hidden_dim), "ep", 1, 1, tiled=True)
        picked = jnp.take(back_rows.reshape(n_rows, hidden_dim), dest_row, axis=0, mode="fill", fill_value=0).reshape(tokens, top_k, hidden_dim)
        routed = jnp.sum(gate_vals[:, :, None] * picked.astype(jnp.float32), axis=1)
        shared = swiglu(hidden, shared_gate, shared_up, shared_down)
        return (shared + routed).astype(jnp.bfloat16)

    return jax.shard_map(device_fn, mesh=mesh, in_specs=(tok_spec, P(), bank_spec, bank_spec, bank_spec, P(), P(), P(), tok_spec, tok_spec), out_specs=tok_spec, check_vma=False)
```

profile of v0, /device:TPU:113, one launch (start us, length us, event | category | flops | bytes accessed | tf_op | source)
XLA Modules:
  0.0 1961.2 jit_solution(13819404711152841500)
XLA Ops:
  0.0 1.0 copy.70
  1.7 0.8 broadcast_compare_fusion
  2.8 0.4 gt.28
  3.2 0.4 gt.27
  4.0 0.4 gt.29
  4.6 18.8 reduce-window.6
  23.4 0.5 slice.14
  23.9 0.6 copy.85
  24.7 0.6 add_add_fusion
  25.3 0.7 fusion.2
  26.6 23.0 %scatter_custom_fusion = s32[12288]{0:T(1024)S(1)} fusion(s32[6144]{0:T(1024)S(1)} %bitcast.48, s32[6144]{0:T(1024)S(1)} %add_select_fusion.3, s32[]{:T(128)} %constant.102.clone.1), kind=kCustom, calls=%fused_computation.60 | custom fusion | bytes 49156 | tf_op jit(solution)/shard_map/scatter | solution.py:50
  49.8 94.1 %gather_fusion = bf16[12288,2048]{1,0:T(8,128)(2,1)} fusion(bf16[1024,2048]{1,0:T(8,128)(2,1)} %param.10, s32[12288]{0:T(1024)S(1)} %fusion.8), kind=kCustom, calls=%fused_computation | custom fusion | bytes 100712448 | tf_op jit(solution)/shard_map/jit(_take)/gather | solution.py:51
  143.9 33.8 %copy_select_fusion = bf16[8,8,192,2048]{3,2,0,1:T(8,128)(2,1)} fusion(bf16[8,8,192,2048]{3,2,1,0:T(8,128)(2,1)} %bitcast.40, pred[8,8,192]{2,0,1:T(8,128)(4,1)S(1)} %copy.80), kind=kLoop, calls=%fused_computation.6 | loop fusion | flops 25165824 | bytes 100675584 | tf_op jit(solution)/shard_map/jit(_take)/select_n | solution.py:51
  177.6 558.7 %all_to_all.10 = bf16[8,8,192,2048]{3,2,0,1:T(8,128)(2,1)} all-to-all(bf16[8,8,192,2048]{3,2,0,1:T(8,128)(2,1)} %copy_select_fusion), channel_id=1, replica_groups=mesh['dp'=4,'ep'=8] {'ep'}, dimensions={1} | all-to-all | bytes 100663296 | tf_op jit(solution)/shard_map/all_to_all | solution.py:52
  736.3 33.4 %copy.82 = bf16[8,8,192,2048]{3,2,1,0:T(8,128)(2,1)} copy(bf16[8,8,192,2048]{3,2,0,1:T(8,128)(2,1)} %all_to_all.10) | data formatting | bytes 100663296 | tf_op jit(solution)/shard_map/all_to_all | solution.py:52
  769.7 87.8 %fusion.28 = f32[8,1536,1408]{2,1,0:T(8,128)} fusion(bf16[8,1536,2048]{2,1,0:T(8,128)(2,1)} %bitcast.41, bf16[8,2048,1408]{2,1,0:T(8,128)(2,1)} %param.12), kind=kOutput, calls=%fused_computation.68 | convolution fusion | flops 70866960384 | bytes 165675008 | tf_op jit(solution)/shard_map/erd,edf->erf/dot_general | solution.py:17
  857.5 94.8 %fusion = bf16[8,1536,1408]{2,1,0:T(8,128)(2,1)} fusion(bf16[8,1536,2048]{2,1,0:T(8,128)(2,1)} %bitcast.42, bf16[8,2048,1408]{2,1,0:T(8,128)(2,1)} %param.13, f32[8,1536,1408]{2,1,0:T(8,128)} %fusion.28), kind=kOutput, calls=%fused_computation.7 | convolution fusion | flops 70970769408 | bytes 200278016 | tf_op jit(solution)/shard_map/erd,edf->erf/dot_general | solution.py:18
  952.3 88.0 %convolution_convert_fusion = bf16[8,1536,2048]{2,1,0:T(8,128)(2,1)} fusion(bf16[8,1536,1408]{2,1,0:T(8,128)(2,1)} %fusion, bf16[8,1408,2048]{2,1,0:T(8,128)(2,1)} %param.14), kind=kOutput, calls=%fused_computation.8 | convolution fusion | flops 70892126208 | bytes 131072000 | tf_op jit(solution)/shard_map/erf,efd->erd/dot_general | solution.py:20
  1040.3 33.4 %copy.83 = bf16[8,8,192,2048]{3,2,0,1:T(8,128)(2,1)} copy(bf16[8,8,192,2048]{3,2,1,0:T(8,128)(2,1)} %bitcast.43) | data formatting | bytes 100663296 | tf_op jit(solution)/shard_map/reshape | solution.py:54
  1073.7 10.0 all-to-all-start.1
  1083.7 0.5 reduce_sum.33
  1084.5 0.9 copy.77
  1086.0 3.6 fusion.26
  1089.7 49.3 %gather_fusion.2 = f32[6144]{0:T(1024)S(1)} fusion(f32[1024,64]{0,1:T(8,128)S(1)} %fusion.6, s32[6144]{0:T(1024)S(1)} %reshape.245), kind=kCustom, calls=%fused_computation.2 | custom fusion | bytes 98304 | tf_op jit(solution)/shard_map/jit(take_along_axis)/gather | solution.py:26
  1139.0 0.5 reshape.248
  1140.0 18.7 fusion.27
  1158.6 468.0 %all-to-all-done.1 = bf16[8,8,192,2048]{3,2,0,1:T(8,128)(2,1)} async-done(((bf16[8,8,192,2048]{3,2,0,1:T(8,128)(2,1)}), bf16[8,8,192,2048]{3,2,0,1:T(8,128)(2,1)}, u32[]{:S(2)}, u32[]{:S(2)}) %all-to-all-start.1) | async-done | bytes 50331680 | tf_op jit(solution)/shard_map/all_to_all | solution.py:54
  1626.6 33.4 %copy.84 = bf16[8,8,192,2048]{3,2,1,0:T(8,128)(2,1)} copy(bf16[8,8,192,2048]{3,2,0,1:T(8,128)(2,1)} %all-to-all-done.1) | data formatting | bytes 100663296 | tf_op jit(solution)/shard_map/all_to_all | solution.py:54
  1660.0 185.0 %gather_fusion.1 = bf16[6144,2048]{1,0:T(8,128)(2,1)} fusion(bf16[12288,2048]{1,0:T(8,128)(2,1)} %bitcast.39, s32[6144]{0:T(1024)S(1)} %broadcast_clamp_fusion), kind=kCustom, calls=%fused_computation.1 | custom fusion | bytes 50356224 | tf_op jit(solution)/shard_map/jit(_take)/gather | solution.py:55
  1845.0 39.5 %gather.20 = bf16[1024,6,2048]{2,1,0:T(8,128)(2,1)} reshape(bf16[6144,2048]{1,0:T(8,128)(2,1)} %gather_fusion.1) | data formatting | bytes 50331648 | tf_op jit(solution)/shard_map/jit(_take)/gather | solution.py:55
  1884.5 39.8 %multiply_reduce_fusion = f32[1024,2048]{1,0:T(8,128)} fusion(bf16[1024,6,2048]{2,1,0:T(8,128)(2,1)} %gather.20, f32[1024,6]{1,0:T(8,128)S(1)} %copy.69, pred[1024,6]{1,0:T(8,128)(4,1)S(1)} %copy-done.1), kind=kLoop, calls=%fused_computation.5 | loop fusion | flops 48234496 | bytes 33585152 | tf_op jit(solution)/shard_map/reduce_sum | solution.py:56
  1924.4 36.3 %add_convert_fusion = bf16[1024,2048]{1,0:T(8,128)(2,1)} fusion(f32[1024,2048]{1,0:T(8,128)} %multiply_reduce_fusion, bf16[2816,2048]{1,0:T(8,128)(2,1)} %param.17, f32[1024,2816]{1,0:T(8,128)} %fusion.27, bf16[1024,2048]{1,0:T(8,128)(2,1)} %param.10, bf16[2048,2816]{1,0:T(8,128)(2,1)} %param.16), kind=kOutput, calls=%fused_computation.10 | convolution fusion | flops 23643815936 | bytes 51380224 | tf_op jit(solution)/shard_map/dot_general | solution.py:13
  (43 shorter events, 3.9 us)
Async XLA Ops:
  0.0 1086.0 %copy-start = (bf16[2048,64]{0,1:T(8,128)(2,1)S(1)}, bf16[2048,64]{0,1:T(8,128)(2,1)}, u32[]{:S(2)}) copy-start(bf16[2048,64]{0,1:T(8,128)(2,1)} %param.11) | copy-start | bytes 786436
  26.0 0.6 copy-start.6
  26.6 117.3 %copy-start.8 = (s32[6144,1]{0,1:T(1,128)}, s32[6144,1]{0,1:T(1,128)S(1)}, u32[]{:S(2)}) copy-start(s32[6144,1]{0,1:T(1,128)S(1)} %compare_select_fusion) | copy-start | bytes 73732
  1073.7 10.0 copy-start.7
  1073.7 10.7 copy-start.2
  1073.7 10.7 copy-start.4
  1073.7 552.9 %all-to-all-start.1 = ((bf16[8,8,192,2048]{3,2,0,1:T(8,128)(2,1)}), bf16[8,8,192,2048]{3,2,0,1:T(8,128)(2,1)}, u32[]{:S(2)}, u32[]{:S(2)}) async-start(bf16[8,8,192,2048]{3,2,0,1:T(8,128)(2,1)} %copy.83), calls=%async_computation.1 | async-start | bytes 100663296 | tf_op jit(solution)/shard_map/all_to_all | solution.py:54
  1089.7 50.0 %copy-start.3 = (s32[1024,6]{0,1:T(8,128)S(1)}, s32[1024,6]{0,1:T(8,128)}, u32[]{:S(2)}) copy-start(s32[1024,6]{0,1:T(8,128)} %param.18) | copy-start | bytes 73732
  1089.7 50.0 %copy-start.5 = (s32[1024,6]{0,1:T(8,128)S(1)}, s32[1024,6]{0,1:T(8,128)}, u32[]{:S(2)}) copy-start(s32[1024,6]{0,1:T(8,128)} %param.19) | copy-start | bytes 73732
  1089.7 50.2 %copy-start.9 = (s32[6144,1]{0,1:T(1,128)S(1)}, s32[6144,1]{0,1:T(1,128)}, u32[]{:S(2)}) copy-start(s32[6144,1]{0,1:T(1,128)} %copy-done.8) | copy-start | bytes 73732
  1845.0 39.5 %copy-start.1 = (pred[1024,6]{1,0:T(8,128)(4,1)S(1)}, pred[1024,6]{1,0:T(8,128)(4,1)}, u32[]{:S(2)}) copy-start(pred[1024,6]{1,0:T(8,128)(4,1)} %copy.77) | copy-start | bytes 18436
where the time goes:
time: 1990 us; the launch traced here: 1960 us
  blocking collectives  559 us (28%)
  local copies, waits for them, and re-layouts  499 us (25%)
  waiting for transfers between devices  468 us (24%)
  matrix products  329 us (17%)
  other arithmetic  95.3 us (5%)
    all_to_all x1, blocking collectives, device_fn(): recv_rows = lax.all_to_all(send_rows, 'ep', 1, 1, tiled=True)  559 us
    all_to_all x1, waiting for transfers between devices, device_fn(): lax.all_to_all(expert_out.reshape(per_dev, groups, capacity, hidden_dim),...  468 us
    gather x2, local copies, waits for them, and re-layouts, device_fn(): jnp.take(back_rows.reshape(n_rows, hidden_dim), dest_row, axis=0, mode='f...  225 us
    dot_general x1, matrix products, expert_bank(): jnp.einsum('erd,edf->erf', tok_rows, up_w, preferred_element_type=jnp.flo...  94.8 us
    gather x1, local copies, waits for them, and re-layouts, device_fn(): jnp.take(hidden, row_token, axis=0, mode='fill', fill_value=0)  94.1 us
    dot_general x1, matrix products, expert_bank(): jnp.einsum('erf,efd->erd', act_rows, down_w, preferred_element_type=jnp.f...  88 us
    dot_general x1, matrix products, expert_bank(): jnp.einsum('erd,edf->erf', tok_rows, gate_w, preferred_element_type=jnp.f...  87.8 us
    gather x5, local copies, waits for them, and re-layouts, route_gates(): jnp.take_along_axis(router_prob, top_idx, axis=1)  50.5 us
  transfers between devices with their start and end apart: 1, of which 1 were waited for; matrix products, arithmetic and copies ran while one was open for 4% of the time, Pallas kernels for 0%

commit v1 on v0

v1 whole, which is shorter than its diff:
```python
import jax
import jax.numpy as jnp
from jax import lax
from jax.experimental import pallas as pl
from jax.experimental.pallas import tpu as pltpu
from jax.sharding import PartitionSpec as P


ROUTE_SCALE = 16.0
LANES = 128


def route_tables(hidden, w_router, top_idx, keep_mask):
    tokens, top_k = top_idx.shape
    experts = w_router.shape[1]
    width, unroll = 256, 4

    def kernel(x_ref, w_ref, idx_ref, keep_ref, tok_ref, gate_ref, slot_t, parts_t):
        logits = jnp.dot(x_ref[...], w_ref[...], preferred_element_type=jnp.float32)
        top = jnp.max(logits, axis=-1, keepdims=True)
        ex = jnp.exp(logits - top)
        prob = ex / jnp.sum(ex, axis=-1, keepdims=True)
        lane = lax.broadcasted_iota(jnp.int32, (tokens, experts), 1)
        member = jnp.zeros((tokens, experts), jnp.float32)
        for k in range(top_k):
            hit = (idx_ref[:, k:k + 1] == lane) & (keep_ref[:, k:k + 1] > 0)
            member = jnp.where(hit, 1.0, member)
        gates = ROUTE_SCALE * prob * member
        before = lax.broadcasted_iota(jnp.int32, (tokens, tokens), 0) >= lax.broadcasted_iota(jnp.int32, (tokens, tokens), 1)
        rank = jnp.dot(jnp.where(before, 1.0, 0.0).astype(jnp.bfloat16), member.astype(jnp.bfloat16), preferred_element_type=jnp.float32)
        slot = jnp.where(member > 0.0, rank - 1.0, -1.0)
        pad = jnp.zeros((tokens, LANES - experts), jnp.float32)
        slot_t[...] = jnp.transpose(jnp.concatenate([slot, pad], axis=1))[:experts]
        gt = jnp.transpose(jnp.concatenate([gates, pad], axis=1))[:experts]
        g1 = gt.astype(jnp.bfloat16).astype(jnp.float32)
        g2 = (gt - g1).astype(jnp.bfloat16).astype(jnp.float32)
        g3 = (gt - g1 - g2).astype(jnp.bfloat16).astype(jnp.float32)
        parts_t[0] = g1
        parts_t[1] = g2
        parts_t[2] = g3
        col = lax.broadcasted_iota(jnp.int32, (8, tokens), 1)
        row = lax.broadcasted_iota(jnp.int32, (8, tokens), 0)
        base = jnp.where(row == 0, (col // 32).astype(jnp.float32), jnp.where(row == 1, (col % 32).astype(jnp.float32), jnp.where(row == 2, 1.0, 0.0)))
        want = lax.broadcasted_iota(jnp.int32, (width, tokens), 0).astype(jnp.float32)

        @pl.loop(0, experts // unroll)
        def _(i):
            for u in range(unroll):
                e = i * unroll + u
                onehot = jnp.where(slot_t[pl.ds(e, 1), :] == want, 1.0, 0.0).astype(jnp.bfloat16)
                vrows = base
                for q in range(3):
                    vrows = jnp.where(row == 3 + q, parts_t[q, pl.ds(e, 1), :], vrows)
                res = lax.dot_general(vrows.astype(jnp.bfloat16), onehot, (((1,), (1,)), ((), ())), preferred_element_type=jnp.float32)
                tok = jnp.where(res[2:3] > 0.5, res[0:1] * 32.0 + res[1:2], float(tokens))
                tok_ref[pl.ds(e, 1), :] = tok
                gate_ref[pl.ds(e, 1), :] = (res[5:6] + res[4:5]) + res[3:4]

    vmem = pl.BlockSpec(memory_space=pltpu.VMEM)
    return pl.pallas_call(
        kernel,
        out_shape=[jax.ShapeDtypeStruct((experts, width), jnp.float32)] * 2,
        in_specs=[vmem] * 4,
        out_specs=[vmem] * 2,
        scratch_shapes=[
            pltpu.VMEM((experts, tokens), jnp.float32),
            pltpu.VMEM((3, experts, tokens), jnp.float32),
        ],
        compiler_params=pltpu.CompilerParams(vmem_limit_bytes=48 * 1024 * 1024),
        cost_estimate=pl.CostEstimate(flops=20_000_000_000, bytes_accessed=8_000_000, transcendentals=100_000),
    )(hidden, w_router, top_idx, keep_mask)


def split(n, parts):
    return [(n * i // parts, n * (i + 1) // parts) for i in range(parts)]


def expert_pass(ids, xa, xb, tok, gate, w1, w3, w2, cap, b_dtype, G=4):
    T, C, L = xa.shape
    E, D, F = w1.shape
    M = 2 * cap
    S = M + 1
    nU, nD = F // 128, D // 256
    base = (2 * T + 2) * C
    narrow = b_dtype == jnp.bfloat16

    def kernel(ids_ref, tok_ref, gate_ref, xa_ref, xb_ref, w1_ref, w3_ref, w2_ref, oa_ref, ob_ref,
               xv, mem, w1v, w3v, w2v, g, av, xsem, wsem, osem):
        first = [ids_ref[0] * E, ids_ref[1] * E]
        x_refs = (xa_ref, xb_ref)

        def weights(e, p):
            return [pltpu.make_async_copy(src.at[e], dst.at[p], wsem.at[p, i]) for i, (src, dst) in enumerate(((w1_ref, w1v), (w3_ref, w3v), (w2_ref, w2v)))]

        def spread(e, b, c):
            t = tok_ref[first[b] + e, c] + b * (T + 1)
            mem[pl.ds(base + b * cap + c, C, stride=S), :] = xv[t].astype(jnp.float32)

        def convert(j):
            g[j] = mem[base + j * S:base + j * S + M, :].astype(jnp.bfloat16)

        def scatter(e, b, cols):
            vals = []
            for c in cols:
                t = tok_ref[first[b] + e, c] + b * (T + 1)
                at = pl.ds(pl.multiple_of(t * C, C), C)
                vals.append((at, mem[at, :] + gate_ref[first[b] + e, c] * mem[pl.ds(base + b * cap + c, C, stride=S), :]))
            for at, v in vals:
                mem[at, :] = v

        loads = [pltpu.make_async_copy(x_refs[b], xv.at[pl.ds(b * (T + 1), T)], xsem.at[b]) for b in range(2)]
        for c in loads: c.start()
        for c in weights(0, 0): c.start(priority=1)
        for b in range(2):
            xv[b * (T + 1) + T] = jnp.zeros((C, L), xv.dtype)

        @pl.loop(0, (2 * T + 2) // 10)
        def _(i):
            mem[pl.ds(pl.multiple_of(i * 10 * C, 8), 10 * C), :] = jnp.zeros((10 * C, L), jnp.float32)

        for b in range(2):
            loads[b].wait()

            @pl.loop(0, cap // 16)
            def _(i):
                for u in range(16):
                    spread(0, b, i * 16 + u)
        for j in range(C): convert(j)

        @pl.loop(0, C)
        def _(i):
            mem[pl.ds(base + i * S, S), :] = jnp.zeros((S, L), jnp.float32)

        def up_tile(p, n):
            cols = pl.ds(n * L, L)
            rows = jnp.concatenate([g[j] for j in range(C)], axis=1)
            h = jnp.dot(rows, jnp.concatenate([w1v[p, :, cols], w3v[p, :, cols]], axis=1), preferred_element_type=jnp.float32)
            av[n] = (jax.nn.silu(h[:, :L]) * h[:, L:]).astype(jnp.bfloat16)

        def down_tile(p, n):
            act = jnp.concatenate([av[j] for j in range(nU)], axis=1)
            h = jnp.dot(act, w2v[p, :, pl.ds(n * 256, 256)], preferred_element_type=jnp.float32)
            h = h.astype(jnp.bfloat16).astype(jnp.float32)
            for k in range(2):
                mem[pl.ds(base + (2 * n + k) * S, M), :] = h[:, L * k:L * k + L]

        groups = [(b, [q + u for u in range(G)]) for b in range(2) for q in range(0, cap, G)]
        parts = split(len(groups), nU)

        @pl.loop(0, E)
        def _(e):
            p = lax.rem(e, 2)
            prev = jnp.maximum(e - 1, 0)
            ahead = jnp.minimum(e + 1, E - 1)
            for c in weights(e, p): c.wait()

            @pl.when(e + 1 < E)
            def _():
                for c in weights(e + 1, 1 - p): c.start(priority=1)

            for n in range(nU):
                for b, cols in groups[slice(*parts[n])]:
                    scatter(prev, b, cols)
                    for c in cols: spread(ahead, b, c)
                up_tile(p, n)
            for n in range(nD):
                convert(2 * n)
                convert(2 * n + 1)
                down_tile(p, n)

        def out(b):
            if b and narrow:
                return pltpu.make_async_copy(xv.at[pl.ds(0, T)], ob_ref, osem.at[b])
            return pltpu.make_async_copy(mem.at[pl.ds(b * (T + 1) * C, T * C)], (oa_ref, ob_ref)[b], osem.at[b])

        for b in range(2):
            @pl.loop(0, cap // 8)
            def _(i):
                scatter(E - 1, b, [i * 8 + u for u in range(8)])

            if b and narrow:
                @pl.loop(0, T // 8)
                def _(i):
                    for u in range(8):
                        r = i * 8 + u
                        xv[r] = mem[pl.ds(pl.multiple_of((T + 1 + r) * C, C), C), :].astype(b_dtype)
            out(b).start()
        for b in range(2):
            out(b).wait()

    anyspec = pl.BlockSpec(memory_space=pl.ANY)
    smem = pl.BlockSpec(memory_space=pltpu.SMEM)
    rows = E * M
    return pl.pallas_call(
        kernel,
        out_shape=[jax.ShapeDtypeStruct((T * C, L), jnp.float32), jax.ShapeDtypeStruct((T, C, L) if narrow else (T * C, L), b_dtype)],
        in_specs=[smem] * 3 + [anyspec] * 5,
        out_specs=[anyspec] * 2,
        scratch_shapes=[
            pltpu.VMEM((2 * T + 2, C, L), jnp.bfloat16),
            pltpu.VMEM((base + C * S, L), jnp.float32),
            pltpu.VMEM((2, D, F), jnp.bfloat16), pltpu.VMEM((2, D, F), jnp.bfloat16), pltpu.VMEM((2, F, D), jnp.bfloat16),
            pltpu.VMEM((C, M, L), jnp.bfloat16),
            pltpu.VMEM((nU, M, L), jnp.bfloat16),
            pltpu.SemaphoreType.DMA((2,)), pltpu.SemaphoreType.DMA((2, 3)), pltpu.SemaphoreType.DMA((2,)),
        ],
        compiler_params=pltpu.CompilerParams(vmem_limit_bytes=67000000),
        cost_estimate=pl.CostEstimate(flops=rows * D * F * 6, bytes_accessed=E * D * F * 6, transcendentals=rows * F),
    )(ids, tok, gate, xa, xb, w1, w3, w2)


def shared_rows(hidden, gate_w, up_w, down_w, total, piece, rows):
    tokens, width = hidden.shape
    ff = gate_w.shape[1]
    tile = 256
    n_up, n_down = ff // tile, width // tile
    up_parts, down_parts = split(n_up, 4), split(n_down, 2)

    def kernel(x_ref, g_ref, u_ref, d_ref, *rest):
        out_ref, xv, gv, uv, dv, act, yv, sem, usem, dsem, osem = rest[-11:]
        load_x = pltpu.make_async_copy(x_ref.at[pl.ds(piece * rows, rows)], xv, sem)
        load_x.start()

        def up_loads(i):
            cols = pl.ds(up_parts[i][0] * tile, (up_parts[i][1] - up_parts[i][0]) * tile)
            return [pltpu.make_async_copy(src.at[:, cols], dst.at[:, cols], usem.at[i, k]) for k, (src, dst) in enumerate(((g_ref, gv), (u_ref, uv)))]

        def down_loads(i):
            cols = pl.ds(down_parts[i][0] * tile, (down_parts[i][1] - down_parts[i][0]) * tile)
            return pltpu.make_async_copy(d_ref.at[:, cols], dv.at[:, cols], dsem.at[i])

        chunks = [up_loads(i) for i in range(len(up_parts))] + [[down_loads(i)] for i in range(len(down_parts))]

        def begin(i):
            if i < len(chunks):
                for c in chunks[i]:
                    c.start()

        def arrive(i):
            for c in chunks[i]:
                c.wait()
            begin(i + 2)

        begin(0)
        load_x.wait()
        begin(1)
        for i, (lo, hi) in enumerate(up_parts):
            arrive(i)
            for n in range(lo, hi):
                cols = slice(n * tile, (n + 1) * tile)
                h_gate = jnp.dot(xv[...], gv[:, cols], preferred_element_type=jnp.float32)
                h_up = jnp.dot(xv[...], uv[:, cols], preferred_element_type=jnp.float32)
                act[:, cols] = (jax.nn.silu(h_gate) * h_up).astype(jnp.bfloat16)

        def store(i):
            cols = pl.ds(down_parts[i][0] * tile, (down_parts[i][1] - down_parts[i][0]) * tile)
            return pltpu.make_async_copy(yv.at[:, cols], out_ref.at[pl.ds(piece * rows, rows), cols], osem.at[i])

        for i, (lo, hi) in enumerate(down_parts):
            arrive(len(up_parts) + i)
            for n in range(lo, hi):
                cols = slice(n * tile, (n + 1) * tile)
                yv[:, cols] = jnp.dot(act[...], dv[:, cols], preferred_element_type=jnp.float32)
            store(i).start()
        for i in range(len(down_parts)):
            store(i).wait()

    operands = [hidden, gate_w, up_w, down_w] + ([] if total is None else [total])
    anyspec = pl.BlockSpec(memory_space=pl.ANY)
    return pl.pallas_call(
        kernel,
        out_shape=jax.ShapeDtypeStruct((tokens, width), jnp.float32),
        in_specs=[anyspec] * len(operands),
        out_specs=anyspec,
        scratch_shapes=[
            pltpu.VMEM((rows, width), jnp.bfloat16),
            pltpu.VMEM((width, ff), jnp.bfloat16), pltpu.VMEM((width, ff), jnp.bfloat16), pltpu.VMEM((ff, width), jnp.bfloat16),
            pltpu.VMEM((rows, ff), jnp.bfloat16), pltpu.VMEM((rows, width), jnp.float32),
            pltpu.SemaphoreType.DMA, pltpu.SemaphoreType.DMA((len(up_parts), 2)), pltpu.SemaphoreType.DMA((len(down_parts),)), pltpu.SemaphoreType.DMA((len(down_parts),)),
        ],
        input_output_aliases={} if total is None else {4: 0},
        compiler_params=pltpu.CompilerParams(vmem_limit_bytes=67000000),
        cost_estimate=pl.CostEstimate(flops=rows * width * ff * 6, bytes_accessed=width * ff * 6, transcendentals=rows * ff),
    )(*operands)


def finish(shared, pa, q, r1, r2, r3):
    tokens, width = shared.shape
    rows = 128
    C = width // LANES
    S = rows + 8

    def kernel(ys_ref, pa_ref, q_ref, r1_ref, r2_ref, r3_ref, out_ref, buf):
        @pl.loop(0, rows // 8)
        def _(i):
            for u in range(8):
                r = i * 8 + u
                v = pa_ref[r]
                for ref in (q_ref, r1_ref, r2_ref, r3_ref):
                    v = v + ref[r].astype(jnp.float32)
                buf[pl.ds(r, C, stride=S), :] = v

        for j in range(C):
            cols = slice(j * LANES, (j + 1) * LANES)
            out_ref[:, cols] = (ys_ref[:, cols] + buf[j * S:j * S + rows, :]).astype(jnp.bfloat16)

    plain = pl.BlockSpec((rows, width), lambda i: (i, 0))
    tile = pl.BlockSpec((rows, C, LANES), lambda i: (i, 0, 0))
    return pl.pallas_call(
        kernel,
        grid=(tokens // rows,),
        out_shape=jax.ShapeDtypeStruct((tokens, width), jnp.bfloat16),
        in_specs=[plain] + [tile] * 5,
        out_specs=plain,
        scratch_shapes=[pltpu.VMEM((C * S, LANES), jnp.float32)],
        compiler_params=pltpu.CompilerParams(vmem_limit_bytes=67000000),
        cost_estimate=pl.CostEstimate(flops=tokens * width * 6, bytes_accessed=tokens * width * 20, transcendentals=0),
    )(shared, pa, q, r1, r2, r3)


def after(value, *deps):
    return lax.optimization_barrier((value, deps))[0]


def solution(mesh):
    n_dev = mesh.shape["ep"]
    chips = n_dev // 2
    tok_spec = P(("dp", "ep"), None)
    bank_spec = P("ep", None, None)
    near = [(2 * c + k, 2 * ((c + (-1 if k == 0 else 1)) % chips) + k) for c in range(chips) for k in range(2)]
    far = [(d, s) for s, d in near]
    across = [(2 * c + k, 2 * ((c + 2) % chips) + k) for c in range(chips) for k in range(2)]
    swap = [(2 * c + k, 2 * c + 1 - k) for c in range(chips) for k in range(2)]

    def device_fn(hidden, w_router, w_gate, w_up, w_down, shared_gate, shared_up, shared_down, top_idx, keep_mask):
        tokens, top_k = top_idx.shape
        width = hidden.shape[1]
        experts = w_router.shape[1]
        per_dev = w_gate.shape[0]
        cap = 8 * ((top_k * tokens + 4 * experts - 1) // (4 * experts))
        me = lax.axis_index("ep")
        chip, core = me // 2, me % 2

        def perm(v, p):
            return lax.ppermute(v, "ep", p)

        x0 = hidden.reshape(tokens, width // LANES, LANES)
        x1 = perm(x0, near)
        tok, gate = route_tables(after(hidden, x0), w_router, top_idx, keep_mask)
        table = jnp.stack([tok, gate], axis=0).reshape(2, n_dev, per_dev, tok.shape[1])
        table = lax.all_to_all(table, "ep", 1, 1, tiled=False)
        table = table.reshape(2, experts, tok.shape[1])[:, :, :cap]
        tok_all, gate_all = table[0].astype(jnp.int32), table[1]

        pieces = 4
        step = tokens // pieces

        def shared_piece(i, total, dep):
            return shared_rows(after(hidden, dep), shared_gate, shared_up, shared_down, total, i, step)

        x0s = perm(x0, swap)
        x1s = perm(x1, swap)
        x3 = perm(x1, near)
        x2 = perm(after(x0, x1), far)
        x3s = perm(x3, swap)
        x2s = perm(x2, swap)

        dirn = jnp.where(core == 0, 1, -1)

        def src(off, k):
            return 2 * ((chip + off + chips) % chips) + k

        def one_pass(xa, xb, off_a, off_b, b_dtype=jnp.float32):
            ids = jnp.stack([src(off_a, core), src(off_b, 1 - core)]).astype(jnp.int32)
            sums = expert_pass(ids, xa, xb, tok_all, gate_all, w_gate, w_up, w_down, cap, b_dtype)
            return [v.reshape(xa.shape) for v in sums]

        def add(pa, q, dep):
            return (after(pa, dep) + q).astype(jnp.bfloat16)

        y = shared_piece(0, None, tok)
        y = shared_piece(1, y, y)
        pa1, pb1 = one_pass(after(x1, y, x1s), x1s, dirn, -dirn)
        q1 = perm(pb1, swap)
        pa2, pb2 = one_pass(after(x3, pa1), x3s, 2, 2)
        q2 = perm(pb2, swap)
        c1 = add(pa1, q1, pa2)
        r1 = perm(c1, far)
        c2 = add(pa2, q2, c1)
        r2 = perm(c2, across)
        pa3, pb3 = one_pass(after(x2, c2), x2s, -dirn, dirn)
        q3 = perm(pb3, swap)
        y = shared_piece(2, y, pa3)
        c3 = add(pa3, q3, y)
        r3 = perm(c3, near)
        pa4, pb4 = one_pass(after(x0, c3), x0s, 0, 0, jnp.bfloat16)
        q4 = perm(pb4, swap)
        y = shared_piece(3, y, (pa4, pb4))
        return finish(y, pa4, q4, r1, r2, r3)

    return jax.shard_map(device_fn, mesh=mesh, in_specs=(tok_spec, P(), bank_spec, bank_spec, bank_spec, P(), P(), P(), tok_spec, tok_spec), out_specs=tok_spec, check_vma=False)
```

time: 1990 us -> 655 us (0.33); the launches traced: 1960 us -> 649 us
  blocking collectives: 559 us -> 0 us
  local copies, waits for them, and re-layouts: 499 us -> 7.46 us
  Pallas kernels: 0 us -> 442 us
  matrix products: 329 us -> 0 us
  waiting for transfers between devices: 468 us -> 148 us
  other arithmetic: 95.3 us -> 30.3 us
    all_to_all x1 -> x0, blocking collectives: 559 us -> none  [device_fn(): recv_rows = lax.all_to_all(send_rows, 'ep', 1, 1, tiled=True)]
    all_to_all x1, waiting for transfers between devices: 468 us -> 0.01 us  [device_fn(): table = lax.all_to_all(table, 'ep', 1, 1, tiled=False)]
    pallas_call x0 -> x10, Pallas kernels: none -> 442 us  [the longest x4 353 us: expert_pass(): pl.pallas_call(kernel, out_shape=[jax.ShapeDtypeStruct((T * C, L), jnp.fl...]
    gather x8 -> x0, local copies, waits for them, and re-layouts: 369 us -> none  [the longest x2 225 us: device_fn(): jnp.take(back_rows.reshape(n_rows, hidden_dim), dest_row, axis=0, mode='f...]
    dot_general x6 -> x0, matrix products: 329 us -> none  [the longest x1 94.8 us: expert_bank(): jnp.einsum('erd,edf->erf', tok_rows, up_w, preferred_element_type=jnp.flo...]
    ppermute x0 -> x14, waiting for transfers between devices: none -> 148 us  [perm(): return lax.ppermute(v, 'ep', p)]
    all_to_all x2 -> x1, local copies, waits for them, and re-layouts: 66.8 us -> 0.91 us  [device_fn(): table = lax.all_to_all(table, 'ep', 1, 1, tiled=False)]
    reduce_sum x3 -> x0, other arithmetic: 40.6 us -> none  [the longest x1 39.8 us: device_fn(): routed = jnp.sum(gate_vals[:, :, None] * picked.astype(jnp.float32), axis=1)]
  transfers between devices with their start and end apart: 1 -> 15, of which waited for: 1 -> 3; matrix products, arithmetic and copies ran while one was open for 4% -> 5% of each run, Pallas kernels for 0% -> 52%
where the time goes in v1:
time: 655 us; the launch traced here: 649 us
  Pallas kernels  442 us (67%)
  waiting for transfers between devices  148 us (23%)
  other arithmetic  30.3 us (5%)
  starting transfers between devices  21.1 us (3%)
  local copies, waits for them, and re-layouts  7.46 us (1%)
    pallas_call x4, Pallas kernels, expert_pass(): pl.pallas_call(kernel, out_shape=[jax.ShapeDtypeStruct((T * C, L), jnp.fl...  353 us
    ppermute x14, waiting for transfers between devices, perm(): return lax.ppermute(v, 'ep', p)  148 us
    pallas_call x4, Pallas kernels, shared_rows(): pl.pallas_call(kernel, out_shape=jax.ShapeDtypeStruct((tokens, width), jn...  59.7 us
    convert_element_type x3, other arithmetic, add(): return (after(pa, dep) + q).astype(jnp.bfloat16)  26.4 us
    pallas_call x1, Pallas kernels, route_tables(): pl.pallas_call(kernel, out_shape=[jax.ShapeDtypeStruct((experts, width),...  14.6 us
    pallas_call x1, Pallas kernels, finish(): pl.pallas_call(kernel, grid=(tokens // rows,), out_shape=jax.ShapeDtypeSt...  14.2 us
    ppermute x14, starting transfers between devices, perm(): return lax.ppermute(v, 'ep', p)  13.7 us
  transfers between devices with their start and end apart: 15, of which 3 were waited for; matrix products, arithmetic and copies ran while one was open for 5% of the time, Pallas kernels for 52%

profile of v1, /device:TPU:113, one launch (start us, length us, event | category | flops | bytes accessed | tf_op | source)
XLA Modules:
  0.0 649.1 jit_solution(18262800362817450036)
XLA Ops:
  0.0 3.6 copy.23
  3.7 1.4 collective-permute-start
  5.1 47.6 %collective-permute-done.xa_ref = bf16[1024,16,128]{2,1,0:T(8,128)(2,1)} collective-permute-done((bf16[1024,16,128]{2,1,0:T(8,128)(2,1)S(1)}, bf16[1024,16,128]{2,1,0:T(8,128)(2,1)}, u32[]{:S(2)}, u32[]{:S(2)}) %collective-permute-start) | collective-permute-done | bytes 4194336 | tf_op jit(solution)/shard_map/ppermute | solution.py:345
  52.6 0.9 collective-permute-start.3
  53.5 0.8 collective-permute-start.2
  55.1 2.2 copy-done
  57.3 14.6 %shard_map.100 = (f32[64,256]{1,0:T(8,128)S(1)}, f32[64,256]{1,0:T(8,128)S(1)}) custom-call(bf16[1024,2048]{1,0:T(8,128)(2,1)S(1)} %copy-done, bf16[2048,64]{1,0:T(8,128)(2,1)S(1)} %copy.17.w_ref, s32[1024,6]{1,0:T(8,128)S(1)} %copy.18.idx_ref, s32[1024,6]{1,0:T(8,128)S(1)} %copy.19.keep_ref), custom_call_target="tpu_custom_call" | custom-call | flops 20000000000 | bytes 8000000 | tf_op jit(solution)/shard_map/pallas_call | solution.py:60
  71.9 0.7 pad_maximum_fusion
  72.5 7.4 %all-to-all-start = ((f32[2,8,8,256]{3,2,0,1:T(8,128)}), f32[2,8,8,256]{3,2,0,1:T(8,128)}, u32[]{:S(2)}, u32[]{:S(2)}) async-start(f32[2,8,8,256]{3,2,0,1:T(8,128)} %pad_maximum_fusion), calls=%async_computation | async-start | bytes 262144 | tf_op jit(solution)/shard_map/all_to_all | solution.py:351
  79.9 14.8 %shard_map.101.rest_0_ = f32[1024,2048]{1,0:T(8,128)} custom-call(bf16[1024,2048]{1,0:T(8,128)(2,1)} %x_ref.4, bf16[2048,2816]{1,0:T(8,128)(2,1)} %g_ref.7, bf16[2048,2816]{1,0:T(8,128)(2,1)} %u_ref.7, bf16[2816,2048]{1,0:T(8,128)(2,1)} %d_ref.7), custom_call_target="tpu_custom_call" | custom-call | flops 8858370048 | bytes 34603008 | tf_op jit(solution)/shard_map/pallas_call | solution.py:270
  94.8 15.1 %shard_map.102.rest_0_ = f32[1024,2048]{1,0:T(8,128)} custom-call(bf16[1024,2048]{1,0:T(8,128)(2,1)} %x_ref.4, bf16[2048,2816]{1,0:T(8,128)(2,1)} %g_ref.7, bf16[2048,2816]{1,0:T(8,128)(2,1)} %u_ref.7, bf16[2816,2048]{1,0:T(8,128)(2,1)} %d_ref.7, f32[1024,2048]{1,0:T(8,128)} %shard_map.101.rest_0_), custom_call_target="tpu_custom_call", output_to_operand_aliasing={{}: (4, {})} | custom-call | flops 8858370048 | bytes 34603008 | tf_op jit(solution)/shard_map/pallas_call | solution.py:270
  109.9 0.7 pad_add_fusion.2.ids_ref
  110.5 0.6 pad_add_fusion.3.ids_ref
  111.1 0.9 copy.25
  112.1 0.7 slice_bitcast_fusion
  113.1 88.7 %shard_map.103 = (f32[16384,128]{1,0:T(8,128)}, f32[16384,128]{1,0:T(8,128)}) custom-call(s32[2]{0:T(128)} %pad_add_fusion.3.ids_ref, s32[64,192]{1,0:T(8,128)} %get-tuple-element.52.tok_ref, f32[64,192]{1,0:T(8,128)} %get-tuple-element.51.gate_ref, bf16[1024,16,128]{2,1,0:T(8,128)(2,1)} %collective-permute-done.xa_ref, ...), custom_call_target="tpu_custom_call" | custom-call | flops 53150220288 | bytes 138412032 | tf_op jit(solution)/shard_map/pallas_call | solution.py:194
  202.1 88.7 %shard_map.104 = (f32[16384,128]{1,0:T(8,128)}, f32[16384,128]{1,0:T(8,128)}) custom-call(s32[2]{0:T(128)} %pad_add_fusion.2.ids_ref, s32[64,192]{1,0:T(8,128)} %get-tuple-element.52.tok_ref, f32[64,192]{1,0:T(8,128)} %get-tuple-element.51.gate_ref, bf16[1024,16,128]{2,1,0:T(8,128)(2,1)} %collective-permute-done.2.xa_ref, ...), custom_call_target="tpu_custom_call" | custom-call | flops 53150220288 | bytes 138412032 | tf_op jit(solution)/shard_map/pallas_call | solution.py:194
  291.2 2.7 collective-permute-start.1
  293.9 45.8 %collective-permute-done.1.xa_ref = bf16[1024,16,128]{2,1,0:T(8,128)(2,1)} collective-permute-done((bf16[1024,16,128]{2,1,0:T(8,128)(2,1)}, bf16[1024,16,128]{2,1,0:T(8,128)(2,1)}, u32[]{:S(2)}, u32[]{:S(2)}) %collective-permute-start.1) | collective-permute-done | bytes 4194336 | tf_op jit(solution)/shard_map/ppermute | solution.py:345
  339.7 1.7 collective-permute-start.7
  341.4 0.7 pad_add_fusion.1.ids_ref
  342.1 8.8 %add_convert_fusion.2 = bf16[1024,16,128]{2,1,0:T(8,128)(2,1)} fusion(f32[1024,16,128]{2,1,0:T(8,128)} %bitcast.34, f32[1024,16,128]{2,1,0:T(8,128)} %collective-permute-done.5), kind=kLoop, calls=%fused_computation.2 | loop fusion | flops 4194304 | bytes 20971520 | tf_op jit(solution)/shard_map/convert_element_type | solution.py:379
  350.9 8.8 %add_convert_fusion.1 = bf16[1024,16,128]{2,1,0:T(8,128)(2,1)} fusion(f32[1024,16,128]{2,1,0:T(8,128)} %bitcast.35, f32[1024,16,128]{2,1,0:T(8,128)} %collective-permute-done.6), kind=kLoop, calls=%fused_computation.1 | loop fusion | flops 4194304 | bytes 20971520 | tf_op jit(solution)/shard_map/convert_element_type | solution.py:379
  359.7 88.7 %shard_map.105 = (f32[16384,128]{1,0:T(8,128)}, f32[16384,128]{1,0:T(8,128)}) custom-call(s32[2]{0:T(128)} %pad_add_fusion.1.ids_ref, s32[64,192]{1,0:T(8,128)} %get-tuple-element.52.tok_ref, f32[64,192]{1,0:T(8,128)} %get-tuple-element.51.gate_ref, bf16[1024,16,128]{2,1,0:T(8,128)(2,1)} %collective-permute-done.1.xa_ref, ...), custom_call_target="tpu_custom_call" | custom-call | flops 53150220288 | bytes 138412032 | tf_op jit(solution)/shard_map/pallas_call | solution.py:194
  449.6 1.7 collective-permute-start.11
  451.7 14.9 %shard_map.106.rest_0_ = f32[1024,2048]{1,0:T(8,128)} custom-call(bf16[1024,2048]{1,0:T(8,128)(2,1)} %x_ref.4, bf16[2048,2816]{1,0:T(8,128)(2,1)} %g_ref.7, bf16[2048,2816]{1,0:T(8,128)(2,1)} %u_ref.7, bf16[2816,2048]{1,0:T(8,128)(2,1)} %d_ref.7, f32[1024,2048]{1,0:T(8,128)} %shard_map.102.rest_0_), custom_call_target="tpu_custom_call", output_to_operand_aliasing={{}: (4, {})} | custom-call | flops 8858370048 | bytes 34603008 | tf_op jit(solution)/shard_map/pallas_call | solution.py:270
  466.6 8.8 %add_convert_fusion = bf16[1024,16,128]{2,1,0:T(8,128)(2,1)} fusion(f32[1024,16,128]{2,1,0:T(8,128)} %bitcast.33, f32[1024,16,128]{2,1,0:T(8,128)} %collective-permute-done.8), kind=kLoop, calls=%fused_computation | loop fusion | flops 4194304 | bytes 20971520 | tf_op jit(solution)/shard_map/convert_element_type | solution.py:379
  475.4 87.4 %shard_map.107 = (f32[16384,128]{1,0:T(8,128)}, bf16[1024,16,128]{2,1,0:T(8,128)(2,1)}) custom-call(s32[2]{0:T(128)} %pad_add_fusion.ids_ref, s32[64,192]{1,0:T(8,128)} %get-tuple-element.52.tok_ref, f32[64,192]{1,0:T(8,128)} %get-tuple-element.51.gate_ref, bf16[1024,16,128]{2,1,0:T(8,128)(2,1)} %bitcast.40, ...), custom_call_target="tpu_custom_call" | custom-call | flops 53150220288 | bytes 138412032 | tf_op jit(solution)/shard_map/pallas_call | solution.py:194
  562.8 1.8 collective-permute-start.10
  565.1 14.9 %shard_map.108.ys_ref = f32[1024,2048]{1,0:T(8,128)} custom-call(bf16[1024,2048]{1,0:T(8,128)(2,1)} %x_ref.4, bf16[2048,2816]{1,0:T(8,128)(2,1)} %g_ref.7, bf16[2048,2816]{1,0:T(8,128)(2,1)} %u_ref.7, bf16[2816,2048]{1,0:T(8,128)(2,1)} %d_ref.7, f32[1024,2048]{1,0:T(8,128)} %shard_map.106.rest_0_), custom_call_target="tpu_custom_call", output_to_operand_aliasing={{}: (4, {})} | custom-call | flops 8858370048 | bytes 34603008 | tf_op jit(solution)/shard_map/pallas_call | solution.py:270
  580.1 54.6 %collective-permute-done.13.r3_ref = bf16[1024,16,128]{2,1,0:T(8,128)(2,1)} collective-permute-done((bf16[1024,16,128]{2,1,0:T(8,128)(2,1)}, bf16[1024,16,128]{2,1,0:T(8,128)(2,1)}, u32[]{:S(2)}, u32[]{:S(2)}) %collective-permute-start.13) | collective-permute-done | bytes 4194336 | tf_op jit(solution)/shard_map/ppermute | solution.py:345
  634.7 14.2 %shard_map.109 = bf16[1024,2048]{1,0:T(8,128)(2,1)} custom-call(f32[1024,2048]{1,0:T(8,128)} %shard_map.108.ys_ref, f32[1024,16,128]{2,1,0:T(8,128)} %bitcast.36, bf16[1024,16,128]{2,1,0:T(8,128)(2,1)} %collective-permute-done.10.q_ref, bf16[1024,16,128]{2,1,0:T(8,128)(2,1)} %collective-permute-done.11.r1_ref, ...), custom_call_target="tpu_custom_call" | custom-call | flops 12582912 | bytes 41943040 | tf_op jit(solution)/shard_map/pallas_call | solution.py:309
  (32 shorter events, 4.1 us)
Async XLA Ops:
  0.0 54.3 %copy-start.2 = (bf16[2048,64]{0,1:T(8,128)(2,1)S(1)}, bf16[2048,64]{0,1:T(8,128)(2,1)}, u32[]{:S(2)}) copy-start(bf16[2048,64]{0,1:T(8,128)(2,1)} %param.11) | copy-start | bytes 786436
  0.0 54.6 %copy-start.3 = (s32[1024,6]{0,1:T(8,128)S(1)}, s32[1024,6]{0,1:T(8,128)}, u32[]{:S(2)}) copy-start(s32[1024,6]{0,1:T(8,128)} %param.18) | copy-start | bytes 73732
  0.0 54.8 %copy-start.4 = (s32[1024,6]{0,1:T(8,128)S(1)}, s32[1024,6]{0,1:T(8,128)}, u32[]{:S(2)}) copy-start(s32[1024,6]{0,1:T(8,128)} %param.19) | copy-start | bytes 73732
  3.6 49.9 %copy-start.1 = (bf16[128,8,16,128]{3,2,1,0:T(8,128)(2,1)}, bf16[128,8,16,128]{3,2,1,0:T(8,128)(2,1)S(1)}, u32[]{:S(2)}) copy-start(bf16[128,8,16,128]{3,2,1,0:T(8,128)(2,1)S(1)} %copy.23) | copy-start | bytes 12582916
  3.7 49.0 %collective-permute-start = (bf16[1024,16,128]{2,1,0:T(8,128)(2,1)S(1)}, bf16[1024,16,128]{2,1,0:T(8,128)(2,1)}, u32[]{:S(2)}, u32[]{:S(2)}) collective-permute-start(bf16[1024,16,128]{2,1,0:T(8,128)(2,1)S(1)} %bitcast.37), channel_id=1, source_target_pairs={{0,6},{1,3},{2,0},{3,5},{4,2},{5,7},{6,4},{7,1},{8,14},{9,11},{10,... | collective-permute-start | bytes 12582920 | tf_op jit(solution)/shard_map/ppermute | solution.py:345
  52.6 60.1 %collective-permute-start.3 = (bf16[1024,16,128]{2,1,0:T(8,128)(2,1)}, bf16[1024,16,128]{2,1,0:T(8,128)(2,1)}, u32[]{:S(2)}, u32[]{:S(2)}) collective-permute-start(bf16[1024,16,128]{2,1,0:T(8,128)(2,1)} %collective-permute-done.xa_ref), channel_id=1, source_target_pairs={{0,1},{1,0},{2,3},{3,2},{4,5},{5,4},{6,7},{7,6},{8,9},{9,8},{10,11... | collective-permute-start | bytes 12582920 | tf_op jit(solution)/shard_map/ppermute | solution.py:345
  53.5 59.2 %collective-permute-start.2 = (bf16[1024,16,128]{2,1,0:T(8,128)(2,1)}, bf16[1024,16,128]{2,1,0:T(8,128)(2,1)}, u32[]{:S(2)}, u32[]{:S(2)}) collective-permute-start(bf16[1024,16,128]{2,1,0:T(8,128)(2,1)} %collective-permute-done.xa_ref), channel_id=1, source_target_pairs={{0,6},{1,3},{2,0},{3,5},{4,2},{5,7},{6,4},{7,1},{8,14},{9,11},{10,... | collective-permute-start | bytes 12582920 | tf_op jit(solution)/shard_map/ppermute | solution.py:345
  55.1 2.2 copy-start
  72.5 38.6 %all-to-all-start = ((f32[2,8,8,256]{3,2,0,1:T(8,128)}), f32[2,8,8,256]{3,2,0,1:T(8,128)}, u32[]{:S(2)}, u32[]{:S(2)}) async-start(f32[2,8,8,256]{3,2,0,1:T(8,128)} %pad_maximum_fusion), calls=%async_computation | async-start | bytes 262144 | tf_op jit(solution)/shard_map/all_to_all | solution.py:351
  112.7 89.4 %collective-permute-start.4 = (bf16[1024,16,128]{2,1,0:T(8,128)(2,1)}, bf16[1024,16,128]{2,1,0:T(8,128)(2,1)}, u32[]{:S(2)}, u32[]{:S(2)}) collective-permute-start(bf16[1024,16,128]{2,1,0:T(8,128)(2,1)} %collective-permute-done.2.xa_ref), channel_id=1, source_target_pairs={{0,1},{1,0},{2,3},{3,2},{4,5},{5,4},{6,7},{7,6},{8,9},{9,8},{10,11... | collective-permute-start | bytes 12582920 | tf_op jit(solution)/shard_map/ppermute | solution.py:345
  201.8 140.3 %collective-permute-start.5 = (f32[1024,16,128]{2,1,0:T(8,128)}, f32[1024,16,128]{2,1,0:T(8,128)}, u32[]{:S(2)}, u32[]{:S(2)}) collective-permute-start(f32[1024,16,128]{2,1,0:T(8,128)} %bitcast.43), channel_id=1, source_target_pairs={{0,1},{1,0},{2,3},{3,2},{4,5},{5,4},{6,7},{7,6},{8,9},{9,8},{10,11... | collective-permute-start | bytes 25165832 | tf_op jit(solution)/shard_map/ppermute | solution.py:345
  290.8 60.1 %collective-permute-start.6 = (f32[1024,16,128]{2,1,0:T(8,128)}, f32[1024,16,128]{2,1,0:T(8,128)}, u32[]{:S(2)}, u32[]{:S(2)}) collective-permute-start(f32[1024,16,128]{2,1,0:T(8,128)} %bitcast.44), channel_id=1, source_target_pairs={{0,1},{1,0},{2,3},{3,2},{4,5},{5,4},{6,7},{7,6},{8,9},{9,8},{10,11... | collective-permute-start | bytes 25165832 | tf_op jit(solution)/shard_map/ppermute | solution.py:345
  291.2 48.5 %collective-permute-start.1 = (bf16[1024,16,128]{2,1,0:T(8,128)(2,1)}, bf16[1024,16,128]{2,1,0:T(8,128)(2,1)}, u32[]{:S(2)}, u32[]{:S(2)}) collective-permute-start(bf16[1024,16,128]{2,1,0:T(8,128)(2,1)} %bitcast.38), channel_id=1, source_target_pairs={{6,0},{3,1},{0,2},{5,3},{2,4},{7,5},{4,6},{1,7},{14,8},{11,9},{8,1... | collective-permute-start | bytes 12582920 | tf_op jit(solution)/shard_map/ppermute | solution.py:345
  339.7 20.0 %collective-permute-start.7 = (bf16[1024,16,128]{2,1,0:T(8,128)(2,1)}, bf16[1024,16,128]{2,1,0:T(8,128)(2,1)}, u32[]{:S(2)}, u32[]{:S(2)}) collective-permute-start(bf16[1024,16,128]{2,1,0:T(8,128)(2,1)} %collective-permute-done.1.xa_ref), channel_id=1, source_target_pairs={{0,1},{1,0},{2,3},{3,2},{4,5},{5,4},{6,7},{7,6},{8,9},{9,8},{10,11... | collective-permute-start | bytes 12582920 | tf_op jit(solution)/shard_map/ppermute | solution.py:345
  448.4 18.2 %collective-permute-start.8 = (f32[1024,16,128]{2,1,0:T(8,128)}, f32[1024,16,128]{2,1,0:T(8,128)}, u32[]{:S(2)}, u32[]{:S(2)}) collective-permute-start(f32[1024,16,128]{2,1,0:T(8,128)} %bitcast.42), channel_id=1, source_target_pairs={{0,1},{1,0},{2,3},{3,2},{4,5},{5,4},{6,7},{7,6},{8,9},{9,8},{10,11... | collective-permute-start | bytes 25165832 | tf_op jit(solution)/shard_map/ppermute | solution.py:345
  448.5 26.9 %collective-permute-start.9 = (bf16[1024,16,128]{2,1,0:T(8,128)(2,1)}, bf16[1024,16,128]{2,1,0:T(8,128)(2,1)}, u32[]{:S(2)}, u32[]{:S(2)}) collective-permute-start(bf16[1024,16,128]{2,1,0:T(8,128)(2,1)} %bitcast.39), channel_id=1, source_target_pairs={{0,1},{1,0},{2,3},{3,2},{4,5},{5,4},{6,7},{7,6},{8,9},{9,8},{10,11... | collective-permute-start | bytes 12582920 | tf_op jit(solution)/shard_map/ppermute | solution.py:345
  449.6 130.5 %collective-permute-start.11 = (bf16[1024,16,128]{2,1,0:T(8,128)(2,1)}, bf16[1024,16,128]{2,1,0:T(8,128)(2,1)}, u32[]{:S(2)}, u32[]{:S(2)}) collective-permute-start(bf16[1024,16,128]{2,1,0:T(8,128)(2,1)} %add_convert_fusion.2), channel_id=1, source_target_pairs={{6,0},{3,1},{0,2},{5,3},{2,4},{7,5},{4,6},{1,7},{14,8},{11,9},{8,1... | collective-permute-start | bytes 12582920 | tf_op jit(solution)/shard_map/ppermute | solution.py:345
  451.3 128.8 %collective-permute-start.12 = (bf16[1024,16,128]{2,1,0:T(8,128)(2,1)}, bf16[1024,16,128]{2,1,0:T(8,128)(2,1)}, u32[]{:S(2)}, u32[]{:S(2)}) collective-permute-start(bf16[1024,16,128]{2,1,0:T(8,128)(2,1)} %add_convert_fusion.1), channel_id=1, source_target_pairs={{0,4},{1,5},{2,6},{3,7},{4,0},{5,1},{6,2},{7,3},{8,12},{9,13},{10,... | collective-permute-start | bytes 12582920 | tf_op jit(solution)/shard_map/ppermute | solution.py:345
  562.8 17.2 %collective-permute-start.10 = (bf16[1024,16,128]{2,1,0:T(8,128)(2,1)}, bf16[1024,16,128]{2,1,0:T(8,128)(2,1)}, u32[]{:S(2)}, u32[]{:S(2)}) collective-permute-start(bf16[1024,16,128]{2,1,0:T(8,128)(2,1)} %get-tuple-element.49), channel_id=1, source_target_pairs={{0,1},{1,0},{2,3},{3,2},{4,5},{5,4},{6,7},{7,6},{8,9},{9,8},{10,11... | collective-permute-start | bytes 12582920 | tf_op jit(solution)/shard_map/ppermute | solution.py:345
  564.6 70.0 %collective-permute-start.13 = (bf16[1024,16,128]{2,1,0:T(8,128)(2,1)}, bf16[1024,16,128]{2,1,0:T(8,128)(2,1)}, u32[]{:S(2)}, u32[]{:S(2)}) collective-permute-start(bf16[1024,16,128]{2,1,0:T(8,128)(2,1)} %add_convert_fusion), channel_id=1, source_target_pairs={{0,6},{1,3},{2,0},{3,5},{4,2},{5,7},{6,4},{7,1},{8,14},{9,11},{10,... | collective-permute-start | bytes 12582920 | tf_op jit(solution)/shard_map/ppermute | solution.py:345

commit v2 on v1

--- a/solution.py
+++ b/solution.py
@@ -82,11 +82,14 @@
     S = M + 1
     nU, nD = F // 128, D // 256
     base = (2 * T + 2) * C
+    mark = -(-(base + C * S) // 8) * 8
     narrow = b_dtype == jnp.bfloat16
 
-    def kernel(ids_ref, tok_ref, gate_ref, xa_ref, xb_ref, w1_ref, w3_ref, w2_ref, oa_ref, ob_ref,
-               xv, mem, w1v, w3v, w2v, g, av, xsem, wsem, osem):
-        first = [ids_ref[0] * E, ids_ref[1] * E]
+    def kernel(ids_ref, tok_all, gate_all, xa_ref, xb_ref, w1_ref, w3_ref, w2_ref, oa_ref, ob_ref,
+               xv, mem, w1v, w3v, w2v, g, av, tok_ref, gate_ref, xsem, wsem, osem, tsem):
+        first = [0, E]
+        lists = [pltpu.make_async_copy(src.at[pl.ds(pl.multiple_of(ids_ref[b] * E, E), E)], dst.at[pl.ds(b * E, E)], tsem.at[b, i]) for b in range(2) for i, (src, dst) in enumerate(((tok_all, tok_ref), (gate_all, gate_ref)))]
+        for c in lists: c.start()
         x_refs = (xa_ref, xb_ref)
 
         def weights(e, p):
@@ -118,6 +121,7 @@
         def _(i):
             mem[pl.ds(pl.multiple_of(i * 10 * C, 8), 10 * C), :] = jnp.zeros((10 * C, L), jnp.float32)
 
+        for c in lists: c.wait()
         for b in range(2):
             loads[b].wait()
 
@@ -131,11 +135,12 @@
         def _(i):
             mem[pl.ds(base + i * S, S), :] = jnp.zeros((S, L), jnp.float32)
 
-        def up_tile(p, n):
+        def up_tile(p, n, lo, hi):
             cols = pl.ds(n * L, L)
-            rows = jnp.concatenate([g[j] for j in range(C)], axis=1)
+            rows = jnp.concatenate([g[j, lo:hi] for j in range(C)], axis=1)
             h = jnp.dot(rows, jnp.concatenate([w1v[p, :, cols], w3v[p, :, cols]], axis=1), preferred_element_type=jnp.float32)
-            av[n] = (jax.nn.silu(h[:, :L]) * h[:, L:]).astype(jnp.bfloat16)
+            av[n, lo:hi] = (jax.nn.silu(h[:, :L]) * h[:, L:]).astype(jnp.bfloat16)
+            mem[pl.ds(mark, 8), :] = h[:8, :L]
 
         def down_tile(p, n):
             act = jnp.concatenate([av[j] for j in range(nU)], axis=1)
@@ -162,7 +167,11 @@
                 for b, cols in groups[slice(*parts[n])]:
                     scatter(prev, b, cols)
                     for c in cols: spread(ahead, b, c)
-                up_tile(p, n)
+                if n > 0:
+                    up_tile(p, n, 0, M)
+                else:
+                    up_tile(p, n, 0, M // 2)
+                    up_tile(p, n, M // 2, M)
             for n in range(nD):
                 convert(2 * n)
                 convert(2 * n + 1)
@@ -194,22 +203,23 @@
     return pl.pallas_call(
         kernel,
         out_shape=[jax.ShapeDtypeStruct((T * C, L), jnp.float32), jax.ShapeDtypeStruct((T, C, L) if narrow else (T * C, L), b_dtype)],
-        in_specs=[smem] * 3 + [anyspec] * 5,
+        in_specs=[smem] + [anyspec] * 7,
         out_specs=[anyspec] * 2,
         scratch_shapes=[
             pltpu.VMEM((2 * T + 2, C, L), jnp.bfloat16),
-            pltpu.VMEM((base + C * S, L), jnp.float32),
+            pltpu.VMEM((mark + 8, L), jnp.float32),
             pltpu.VMEM((2, D, F), jnp.bfloat16), pltpu.VMEM((2, D, F), jnp.bfloat16), pltpu.VMEM((2, F, D), jnp.bfloat16),
             pltpu.VMEM((C, M, L), jnp.bfloat16),
             pltpu.VMEM((nU, M, L), jnp.bfloat16),
-            pltpu.SemaphoreType.DMA((2,)), pltpu.SemaphoreType.DMA((2, 3)), pltpu.SemaphoreType.DMA((2,)),
+            pltpu.SMEM((2 * E, tok.shape[1]), jnp.int32), pltpu.SMEM((2 * E, tok.shape[1]), jnp.float32),
+            pltpu.SemaphoreType.DMA((2,)), pltpu.SemaphoreType.DMA((2, 3)), pltpu.SemaphoreType.DMA((2,)), pltpu.SemaphoreType.DMA((2, 2)),
         ],
         compiler_params=pltpu.CompilerParams(vmem_limit_bytes=67000000),
         cost_estimate=pl.CostEstimate(flops=rows * D * F * 6, bytes_accessed=E * D * F * 6, transcendentals=rows * F),
     )(ids, tok, gate, xa, xb, w1, w3, w2)
 
 
-def shared_rows(hidden, gate_w, up_w, down_w, total, piece, rows):
+def shared_rows(hidden, gate_w, up_w, down_w, total, row0, rows):
     tokens, width = hidden.shape
     ff = gate_w.shape[1]
     tile = 256
@@ -218,7 +228,7 @@
 
     def kernel(x_ref, g_ref, u_ref, d_ref, *rest):
         out_ref, xv, gv, uv, dv, act, yv, sem, usem, dsem, osem = rest[-11:]
-        load_x = pltpu.make_async_copy(x_ref.at[pl.ds(piece * rows, rows)], xv, sem)
+        load_x = pltpu.make_async_copy(x_ref.at[pl.ds(row0, rows)], xv, sem)
         load_x.start()
 
         def up_loads(i):
@@ -254,7 +264,7 @@
 
         def store(i):
             cols = pl.ds(down_parts[i][0] * tile, (down_parts[i][1] - down_parts[i][0]) * tile)
-            return pltpu.make_async_copy(yv.at[:, cols], out_ref.at[pl.ds(piece * rows, rows), cols], osem.at[i])
+            return pltpu.make_async_copy(yv.at[:, cols], out_ref.at[pl.ds(row0, rows), cols], osem.at[i])
 
         for i, (lo, hi) in enumerate(down_parts):
             arrive(len(up_parts) + i)
@@ -286,36 +296,104 @@
 
 def finish(shared, pa, q, r1, r2, r3):
     tokens, width = shared.shape
-    rows = 128
+    n, depth = 16, 6
+    rows = tokens // n
     C = width // LANES
-    S = rows + 8
-
-    def kernel(ys_ref, pa_ref, q_ref, r1_ref, r2_ref, r3_ref, out_ref, buf):
-        @pl.loop(0, rows // 8)
-        def _(i):
-            for u in range(8):
-                r = i * 8 + u
-                v = pa_ref[r]
-                for ref in (q_ref, r1_ref, r2_ref, r3_ref):
-                    v = v + ref[r].astype(jnp.float32)
-                buf[pl.ds(r, C, stride=S), :] = v
-
-        for j in range(C):
-            cols = slice(j * LANES, (j + 1) * LANES)
-            out_ref[:, cols] = (ys_ref[:, cols] + buf[j * S:j * S + rows, :]).astype(jnp.bfloat16)
-
-    plain = pl.BlockSpec((rows, width), lambda i: (i, 0))
-    tile = pl.BlockSpec((rows, C, LANES), lambda i: (i, 0, 0))
+    S = rows + 1
+
+    def kernel(ys_ref, pa_ref, q_ref, r1_ref, r2_ref, r3_ref, out_ref, yv, pv, rv, ov, buf, lsem, osem):
+        def loads(i):
+            part = pl.ds(i * rows, rows)
+            copies = [(ys_ref.at[part], yv.at[part]), (pa_ref.at[part], pv.at[part])]
+            copies += [(src.at[part], rv.at[k, part]) for k, src in enumerate((q_ref, r1_ref, r2_ref, r3_ref))]
+            return [pltpu.make_async_copy(src, dst, lsem.at[i, k]) for k, (src, dst) in enumerate(copies)]
+
+        def store(i):
+            part = pl.ds(i * rows, rows)
+            return pltpu.make_async_copy(ov.at[part], out_ref.at[part], osem.at[i])
+
+        for i in range(depth):
+            for c in loads(i): c.start()
+        for i in range(n):
+            for c in loads(i): c.wait()
+            if i + depth < n:
+                for c in loads(i + depth): c.start()
+
+            @pl.loop(0, rows // 8)
+            def _(k):
+                for u in range(8):
+                    r = i * rows + k * 8 + u
+                    v = pv[r]
+                    for t in range(4):
+                        v = v + rv[t, r].astype(jnp.float32)
+                    buf[pl.ds(k * 8 + u, C, stride=S), :] = v
+
+            for j in range(C):
+                at, cols = slice(i * rows, (i + 1) * rows), slice(j * LANES, (j + 1) * LANES)
+                ov[at, cols] = (yv[at, cols] + buf[j * S:j * S + rows, :]).astype(jnp.bfloat16)
+            store(i).start()
+        for i in range(n):
+            store(i).wait()
+
+    anyspec = pl.BlockSpec(memory_space=pl.ANY)
     return pl.pallas_call(
         kernel,
-        grid=(tokens // rows,),
         out_shape=jax.ShapeDtypeStruct((tokens, width), jnp.bfloat16),
-        in_specs=[plain] + [tile] * 5,
-        out_specs=plain,
-        scratch_shapes=[pltpu.VMEM((C * S, LANES), jnp.float32)],
+        in_specs=[anyspec] * 6,
+        out_specs=anyspec,
+        scratch_shapes=[
+            pltpu.VMEM((tokens, width), jnp.float32), pltpu.VMEM(pa.shape, jnp.float32), pltpu.VMEM((4,) + q.shape, jnp.bfloat16),
+            pltpu.VMEM((tokens, width), jnp.bfloat16), pltpu.VMEM((C * S, LANES), jnp.float32),
+            pltpu.SemaphoreType.DMA((n, 6)), pltpu.SemaphoreType.DMA((n,)),
+        ],
         compiler_params=pltpu.CompilerParams(vmem_limit_bytes=67000000),
         cost_estimate=pl.CostEstimate(flops=tokens * width * 6, bytes_accessed=tokens * width * 20, transcendentals=0),
     )(shared, pa, q, r1, r2, r3)
+
+
+def add_partials(pa, q):
+    tokens, C, L = pa.shape
+    n, depth = 16, 6
+    rows = tokens // n
+
+    def kernel(a_ref, q_ref, out_ref, av, qv, cv, asem, qsem, csem):
+        part = [pl.ds(i * rows, rows) for i in range(n)]
+
+        def loads(i):
+            return [pltpu.make_async_copy(a_ref.at[part[i]], av.at[part[i]], asem.at[i]), pltpu.make_async_copy(q_ref.at[part[i]], qv.at[part[i]], qsem.at[i])]
+
+        def store(i):
+            return pltpu.make_async_copy(cv.at[part[i]], out_ref.at[part[i]], csem.at[i])
+
+        for i in range(depth):
+            for c in loads(i): c.start()
+        for i in range(n):
+            for c in loads(i): c.wait()
+            if i + depth < n:
+                for c in loads(i + depth): c.start()
+
+            @pl.loop(0, rows // 8)
+            def _(k):
+                at = pl.ds(i * rows + k * 8, 8)
+                cv[at] = (av[at] + qv[at]).astype(jnp.bfloat16)
+
+            store(i).start()
+        for i in range(n):
+            store(i).wait()
+
+    anyspec = pl.BlockSpec(memory_space=pl.ANY)
+    return pl.pallas_call(
+        kernel,
+        out_shape=jax.ShapeDtypeStruct(pa.shape, jnp.bfloat16),
+        in_specs=[anyspec] * 2,
+        out_specs=anyspec,
+        scratch_shapes=[
+            pltpu.VMEM(pa.shape, jnp.float32), pltpu.VMEM(pa.shape, jnp.float32), pltpu.VMEM(pa.shape, jnp.bfloat16),
+            pltpu.SemaphoreType.DMA((n,)), pltpu.SemaphoreType.DMA((n,)), pltpu.SemaphoreType.DMA((n,)),
+        ],
+        compiler_params=pltpu.CompilerParams(vmem_limit_bytes=67000000),
+        cost_estimate=pl.CostEstimate(flops=tokens * C * L, bytes_accessed=tokens * C * L * 10, transcendentals=0),
+    )(pa, q)
 
 
 def after(value, *deps):
@@ -349,21 +427,16 @@
         tok, gate = route_tables(after(hidden, x0), w_router, top_idx, keep_mask)
         table = jnp.stack([tok, gate], axis=0).reshape(2, n_dev, per_dev, tok.shape[1])
         table = lax.all_to_all(table, "ep", 1, 1, tiled=False)
-        table = table.reshape(2, experts, tok.shape[1])[:, :, :cap]
+        table = table.reshape(2, experts, tok.shape[1])
         tok_all, gate_all = table[0].astype(jnp.int32), table[1]
 
-        pieces = 4
-        step = tokens // pieces
-
-        def shared_piece(i, total, dep):
-            return shared_rows(after(hidden, dep), shared_gate, shared_up, shared_down, total, i, step)
+        def shared_piece(total, dep, lo, hi):
+            return shared_rows(after(hidden, dep), shared_gate, shared_up, shared_down, total, lo * tokens // 4, (hi - lo) * tokens // 4)
 
         x0s = perm(x0, swap)
         x1s = perm(x1, swap)
         x3 = perm(x1, near)
-        x2 = perm(after(x0, x1), far)
         x3s = perm(x3, swap)
-        x2s = perm(x2, swap)
 
         dirn = jnp.where(core == 0, 1, -1)
 
@@ -376,11 +449,12 @@
             return [v.reshape(xa.shape) for v in sums]
 
         def add(pa, q, dep):
-            return (after(pa, dep) + q).astype(jnp.bfloat16)
-
-        y = shared_piece(0, None, tok)
-        y = shared_piece(1, y, y)
+            return add_partials(after(pa, dep), q)
+
+        y = shared_piece(None, tok, 0, 2)
         pa1, pb1 = one_pass(after(x1, y, x1s), x1s, dirn, -dirn)
+        x2 = perm(after(x0, pa1), far)
+        x2s = perm(x2, swap)
         q1 = perm(pb1, swap)
         pa2, pb2 = one_pass(after(x3, pa1), x3s, 2, 2)
         q2 = perm(pb2, swap)
@@ -390,12 +464,12 @@
         r2 = perm(c2, across)
         pa3, pb3 = one_pass(after(x2, c2), x2s, -dirn, dirn)
         q3 = perm(pb3, swap)
-        y = shared_piece(2, y, pa3)
+        y = shared_piece(y, pa3, 2, 3)
         c3 = add(pa3, q3, y)
         r3 = perm(c3, near)
         pa4, pb4 = one_pass(after(x0, c3), x0s, 0, 0, jnp.bfloat16)
         q4 = perm(pb4, swap)
-        y = shared_piece(3, y, (pa4, pb4))
+        y = shared_piece(y, (pa4, pb4), 3, 4)
         return finish(y, pa4, q4, r1, r2, r3)
 
     return jax.shard_map(device_fn, mesh=mesh, in_specs=(tok_spec, P(), bank_spec, bank_spec, bank_spec, P(), P(), P(), tok_spec, tok_spec), out_specs=tok_spec, check_vma=False)

time: 655 us -> 619 us (0.945)
  other arithmetic: 30.3 us -> 4.7 us
  Pallas kernels: 442 us -> 420 us
  waiting for transfers between devices: 148 us -> 159 us
    pallas_call x4, Pallas kernels: 353 us -> 314 us  [expert_pass(): pl.pallas_call(kernel, out_shape=[jax.ShapeDtypeStruct((T * C, L), jnp.fl...]
    convert_element_type x3 -> x0, other arithmetic: 26.4 us -> none  [add(): return (after(pa, dep) + q).astype(jnp.bfloat16)]
    pallas_call x1 -> x4, Pallas kernels: 14.2 us -> 38.7 us  [the longest x3 24.9 us: add_partials(): pl.pallas_call(kernel, out_shape=jax.ShapeDtypeStruct(pa.shape, jnp.bfloa...]
    ppermute x14, waiting for transfers between devices: 148 us -> 158 us  [perm(): return lax.ppermute(v, 'ep', p)]
    pallas_call x4 -> x3, Pallas kernels: 59.7 us -> 53.4 us  [shared_rows(): pl.pallas_call(kernel, out_shape=jax.ShapeDtypeStruct((tokens, width), jn...]
  transfers between devices with their start and end apart: 15 -> 15, of which waited for: 3 -> 4; matrix products, arithmetic and copies ran while one was open for 5% -> 1% of each run, Pallas kernels for 52% -> 53%
where the time goes in v2:
time: 619 us; the launch traced here: 613 us
  Pallas kernels  420 us (68%)
  waiting for transfers between devices  159 us (26%)
  starting transfers between devices  21.6 us (3%)
  local copies, waits for them, and re-layouts  6.54 us (1%)
    pallas_call x4, Pallas kernels, expert_pass(): pl.pallas_call(kernel, out_shape=[jax.ShapeDtypeStruct((T * C, L), jnp.fl...  314 us
    ppermute x14, waiting for transfers between devices, perm(): return lax.ppermute(v, 'ep', p)  158 us
    pallas_call x3, Pallas kernels, shared_rows(): pl.pallas_call(kernel, out_shape=jax.ShapeDtypeStruct((tokens, width), jn...  53.4 us
    pallas_call x3, Pallas kernels, add_partials(): pl.pallas_call(kernel, out_shape=jax.ShapeDtypeStruct(pa.shape, jnp.bfloa...  24.9 us
    pallas_call x1, Pallas kernels, route_tables(): pl.pallas_call(kernel, out_shape=[jax.ShapeDtypeStruct((experts, width),...  14.6 us
    ppermute x14, starting transfers between devices, perm(): return lax.ppermute(v, 'ep', p)  14.5 us
    pallas_call x1, Pallas kernels, finish(): pl.pallas_call(kernel, out_shape=jax.ShapeDtypeStruct((tokens, width), jn...  13.9 us
  transfers between devices with their start and end apart: 15, of which 4 were waited for; matrix products, arithmetic and copies ran while one was open for 1% of the time, Pallas kernels for 53%

profile of v2, /device:TPU:113, one launch (start us, length us, event | category | flops | bytes accessed | tf_op | source)
XLA Modules:
  0.0 613.3 jit_solution(12156049631189492711)
XLA Ops:
  0.0 3.6 copy.21
  3.7 1.4 collective-permute-start
  5.1 47.6 %collective-permute-done.xa_ref = bf16[1024,16,128]{2,1,0:T(8,128)(2,1)} collective-permute-done((bf16[1024,16,128]{2,1,0:T(8,128)(2,1)S(1)}, bf16[1024,16,128]{2,1,0:T(8,128)(2,1)}, u32[]{:S(2)}, u32[]{:S(2)}) %collective-permute-start) | collective-permute-done | bytes 4194336 | tf_op jit(solution)/shard_map/ppermute | solution.py:423
  52.6 0.9 collective-permute-start.1
  53.5 0.8 collective-permute-start.3
  55.1 2.2 copy-done
  57.3 14.6 %shard_map.100 = (f32[64,256]{1,0:T(8,128)S(1)}, f32[64,256]{1,0:T(8,128)S(1)}) custom-call(bf16[1024,2048]{1,0:T(8,128)(2,1)S(1)} %copy-done, bf16[2048,64]{1,0:T(8,128)(2,1)S(1)} %copy.16.w_ref, s32[1024,6]{1,0:T(8,128)S(1)} %copy.17.idx_ref, s32[1024,6]{1,0:T(8,128)S(1)} %copy.18.keep_ref), custom_call_target="tpu_custom_call" | custom-call | flops 20000000000 | bytes 8000000 | tf_op jit(solution)/shard_map/pallas_call | solution.py:60
  71.9 0.7 pad_maximum_fusion
  72.5 7.1 %all-to-all-start = ((f32[2,8,8,256]{3,2,0,1:T(8,128)}), f32[2,8,8,256]{3,2,0,1:T(8,128)}, u32[]{:S(2)}, u32[]{:S(2)}) async-start(f32[2,8,8,256]{3,2,0,1:T(8,128)} %pad_maximum_fusion), calls=%async_computation | async-start | bytes 262144 | tf_op jit(solution)/shard_map/all_to_all | solution.py:429
  79.7 23.6 %shard_map.101.rest_0_ = f32[1024,2048]{1,0:T(8,128)} custom-call(bf16[1024,2048]{1,0:T(8,128)(2,1)} %x_ref.3, bf16[2048,2816]{1,0:T(8,128)(2,1)} %g_ref.5, bf16[2048,2816]{1,0:T(8,128)(2,1)} %u_ref.5, bf16[2816,2048]{1,0:T(8,128)(2,1)} %d_ref.5), custom_call_target="tpu_custom_call" | custom-call | flops 17716740096 | bytes 34603008 | tf_op jit(solution)/shard_map/pallas_call | solution.py:280
  104.5 1.4 all-to-all-done
  105.9 1.5 slice_bitcast_fusion
  107.6 78.7 %shard_map.102 = (f32[16384,128]{1,0:T(8,128)}, f32[16384,128]{1,0:T(8,128)}) custom-call(s32[2]{0:T(128)} %pad_add_fusion.2.ids_ref, s32[64,256]{1,0:T(8,128)} %get-tuple-element.50.tok_all, f32[64,256]{1,0:T(8,128)} %get-tuple-element.49.gate_all, bf16[1024,16,128]{2,1,0:T(8,128)(2,1)} %collective-permute-done.xa_ref, ...), custom_call_target="tpu_custom_call" | custom-call | flops 53150220288 | bytes 138412032 | tf_op jit(solution)/shard_map/pallas_call | solution.py:203
  186.4 0.7 collective-permute-start.5
  187.1 78.7 %shard_map.103 = (f32[16384,128]{1,0:T(8,128)}, f32[16384,128]{1,0:T(8,128)}) custom-call(s32[2]{0:T(128)} %pad_add_fusion.3.ids_ref, s32[64,256]{1,0:T(8,128)} %get-tuple-element.50.tok_all, f32[64,256]{1,0:T(8,128)} %get-tuple-element.49.gate_all, bf16[1024,16,128]{2,1,0:T(8,128)(2,1)} %collective-permute-done.3.xa_ref, ...), custom_call_target="tpu_custom_call" | custom-call | flops 53150220288 | bytes 138412032 | tf_op jit(solution)/shard_map/pallas_call | solution.py:203
  266.2 2.3 collective-permute-start.2
  268.5 45.8 %collective-permute-done.2.xa_ref = bf16[1024,16,128]{2,1,0:T(8,128)(2,1)} collective-permute-done((bf16[1024,16,128]{2,1,0:T(8,128)(2,1)}, bf16[1024,16,128]{2,1,0:T(8,128)(2,1)}, u32[]{:S(2)}, u32[]{:S(2)}) %collective-permute-start.2) | collective-permute-done | bytes 4194336 | tf_op jit(solution)/shard_map/ppermute | solution.py:423
  314.3 2.2 collective-permute-start.7
  316.4 0.7 pad_add_fusion.1.ids_ref
  317.1 8.3 %shard_map.104 = bf16[1024,16,128]{2,1,0:T(8,128)(2,1)} custom-call(f32[1024,16,128]{2,1,0:T(8,128)} %bitcast.31, f32[1024,16,128]{2,1,0:T(8,128)} %collective-permute-done.5.q_ref), custom_call_target="tpu_custom_call" | custom-call | flops 2097152 | bytes 20971520 | tf_op jit(solution)/shard_map/pallas_call | solution.py:385
  325.4 8.3 %shard_map.105 = bf16[1024,16,128]{2,1,0:T(8,128)(2,1)} custom-call(f32[1024,16,128]{2,1,0:T(8,128)} %bitcast.32, f32[1024,16,128]{2,1,0:T(8,128)} %collective-permute-done.6.q_ref), custom_call_target="tpu_custom_call" | custom-call | flops 2097152 | bytes 20971520 | tf_op jit(solution)/shard_map/pallas_call | solution.py:385
  333.7 78.8 %shard_map.106 = (f32[16384,128]{1,0:T(8,128)}, f32[16384,128]{1,0:T(8,128)}) custom-call(s32[2]{0:T(128)} %pad_add_fusion.1.ids_ref, s32[64,256]{1,0:T(8,128)} %get-tuple-element.50.tok_all, f32[64,256]{1,0:T(8,128)} %get-tuple-element.49.gate_all, bf16[1024,16,128]{2,1,0:T(8,128)(2,1)} %collective-permute-done.2.xa_ref, ...), custom_call_target="tpu_custom_call" | custom-call | flops 53150220288 | bytes 138412032 | tf_op jit(solution)/shard_map/pallas_call | solution.py:203
  413.1 0.7 pad_add_fusion.ids_ref
  413.8 1.5 collective-permute-start.11
  415.3 14.9 %shard_map.107.rest_0_ = f32[1024,2048]{1,0:T(8,128)} custom-call(bf16[1024,2048]{1,0:T(8,128)(2,1)} %x_ref.3, bf16[2048,2816]{1,0:T(8,128)(2,1)} %g_ref.5, bf16[2048,2816]{1,0:T(8,128)(2,1)} %u_ref.5, bf16[2816,2048]{1,0:T(8,128)(2,1)} %d_ref.5, f32[1024,2048]{1,0:T(8,128)} %shard_map.101.rest_0_), custom_call_target="tpu_custom_call", output_to_operand_aliasing={{}: (4, {})} | custom-call | flops 8858370048 | bytes 34603008 | tf_op jit(solution)/shard_map/pallas_call | solution.py:280
  430.2 8.3 %shard_map.108 = bf16[1024,16,128]{2,1,0:T(8,128)(2,1)} custom-call(f32[1024,16,128]{2,1,0:T(8,128)} %bitcast.30, f32[1024,16,128]{2,1,0:T(8,128)} %collective-permute-done.8.q_ref), custom_call_target="tpu_custom_call" | custom-call | flops 2097152 | bytes 20971520 | tf_op jit(solution)/shard_map/pallas_call | solution.py:385
  438.5 77.5 %shard_map.109 = (f32[16384,128]{1,0:T(8,128)}, bf16[1024,16,128]{2,1,0:T(8,128)(2,1)}) custom-call(s32[2]{0:T(128)} %pad_add_fusion.ids_ref, s32[64,256]{1,0:T(8,128)} %get-tuple-element.50.tok_all, f32[64,256]{1,0:T(8,128)} %get-tuple-element.49.gate_all, bf16[1024,16,128]{2,1,0:T(8,128)(2,1)} %bitcast.37, ...), custom_call_target="tpu_custom_call" | custom-call | flops 53150220288 | bytes 138412032 | tf_op jit(solution)/shard_map/pallas_call | solution.py:203
  516.0 2.6 collective-permute-start.10
  518.5 0.9 collective-permute-start.13
  519.5 14.9 %shard_map.110.ys_ref = f32[1024,2048]{1,0:T(8,128)} custom-call(bf16[1024,2048]{1,0:T(8,128)(2,1)} %x_ref.3, bf16[2048,2816]{1,0:T(8,128)(2,1)} %g_ref.5, bf16[2048,2816]{1,0:T(8,128)(2,1)} %u_ref.5, bf16[2816,2048]{1,0:T(8,128)(2,1)} %d_ref.5, f32[1024,2048]{1,0:T(8,128)} %shard_map.107.rest_0_), custom_call_target="tpu_custom_call", output_to_operand_aliasing={{}: (4, {})} | custom-call | flops 8858370048 | bytes 34603008 | tf_op jit(solution)/shard_map/pallas_call | solution.py:280
  534.4 64.5 %collective-permute-done.13.r3_ref = bf16[1024,16,128]{2,1,0:T(8,128)(2,1)} collective-permute-done((bf16[1024,16,128]{2,1,0:T(8,128)(2,1)}, bf16[1024,16,128]{2,1,0:T(8,128)(2,1)}, u32[]{:S(2)}, u32[]{:S(2)}) %collective-permute-start.13) | collective-permute-done | bytes 4194336 | tf_op jit(solution)/shard_map/ppermute | solution.py:423
  598.9 13.9 %shard_map.111 = bf16[1024,2048]{1,0:T(8,128)(2,1)} custom-call(f32[1024,2048]{1,0:T(8,128)} %shard_map.110.ys_ref, f32[1024,16,128]{2,1,0:T(8,128)} %bitcast.33, bf16[1024,16,128]{2,1,0:T(8,128)(2,1)} %collective-permute-done.10.q_ref, bf16[1024,16,128]{2,1,0:T(8,128)(2,1)} %collective-permute-done.11.r1_ref, ...), custom_call_target="tpu_custom_call" | custom-call | flops 12582912 | bytes 41943040 | tf_op jit(solution)/shard_map/pallas_call | solution.py:339
  (30 shorter events, 3.2 us)
Async XLA Ops:
  0.0 54.3 %copy-start.2 = (bf16[2048,64]{0,1:T(8,128)(2,1)S(1)}, bf16[2048,64]{0,1:T(8,128)(2,1)}, u32[]{:S(2)}) copy-start(bf16[2048,64]{0,1:T(8,128)(2,1)} %param.11) | copy-start | bytes 786436
  0.0 54.6 %copy-start.3 = (s32[1024,6]{0,1:T(8,128)S(1)}, s32[1024,6]{0,1:T(8,128)}, u32[]{:S(2)}) copy-start(s32[1024,6]{0,1:T(8,128)} %param.18) | copy-start | bytes 73732
  0.0 54.8 %copy-start.4 = (s32[1024,6]{0,1:T(8,128)S(1)}, s32[1024,6]{0,1:T(8,128)}, u32[]{:S(2)}) copy-start(s32[1024,6]{0,1:T(8,128)} %param.19) | copy-start | bytes 73732
  3.6 49.9 %copy-start.1 = (bf16[128,8,16,128]{3,2,1,0:T(8,128)(2,1)}, bf16[128,8,16,128]{3,2,1,0:T(8,128)(2,1)S(1)}, u32[]{:S(2)}) copy-start(bf16[128,8,16,128]{3,2,1,0:T(8,128)(2,1)S(1)} %copy.21) | copy-start | bytes 12582916
  3.7 49.0 %collective-permute-start = (bf16[1024,16,128]{2,1,0:T(8,128)(2,1)S(1)}, bf16[1024,16,128]{2,1,0:T(8,128)(2,1)}, u32[]{:S(2)}, u32[]{:S(2)}) collective-permute-start(bf16[1024,16,128]{2,1,0:T(8,128)(2,1)S(1)} %bitcast.34), channel_id=1, source_target_pairs={{0,6},{1,3},{2,0},{3,5},{4,2},{5,7},{6,4},{7,1},{8,14},{9,11},{10,... | collective-permute-start | bytes 12582920 | tf_op jit(solution)/shard_map/ppermute | solution.py:423
  52.6 54.7 %collective-permute-start.1 = (bf16[1024,16,128]{2,1,0:T(8,128)(2,1)}, bf16[1024,16,128]{2,1,0:T(8,128)(2,1)}, u32[]{:S(2)}, u32[]{:S(2)}) collective-permute-start(bf16[1024,16,128]{2,1,0:T(8,128)(2,1)} %collective-permute-done.xa_ref), channel_id=1, source_target_pairs={{0,1},{1,0},{2,3},{3,2},{4,5},{5,4},{6,7},{7,6},{8,9},{9,8},{10,11... | collective-permute-start | bytes 12582920 | tf_op jit(solution)/shard_map/ppermute | solution.py:423
  53.5 53.8 %collective-permute-start.3 = (bf16[1024,16,128]{2,1,0:T(8,128)(2,1)}, bf16[1024,16,128]{2,1,0:T(8,128)(2,1)}, u32[]{:S(2)}, u32[]{:S(2)}) collective-permute-start(bf16[1024,16,128]{2,1,0:T(8,128)(2,1)} %collective-permute-done.xa_ref), channel_id=1, source_target_pairs={{0,6},{1,3},{2,0},{3,5},{4,2},{5,7},{6,4},{7,1},{8,14},{9,11},{10,... | collective-permute-start | bytes 12582920 | tf_op jit(solution)/shard_map/ppermute | solution.py:423
  55.1 2.2 copy-start
  72.5 33.3 %all-to-all-start = ((f32[2,8,8,256]{3,2,0,1:T(8,128)}), f32[2,8,8,256]{3,2,0,1:T(8,128)}, u32[]{:S(2)}, u32[]{:S(2)}) async-start(f32[2,8,8,256]{3,2,0,1:T(8,128)} %pad_maximum_fusion), calls=%async_computation | async-start | bytes 262144 | tf_op jit(solution)/shard_map/all_to_all | solution.py:429
  107.4 79.7 %collective-permute-start.4 = (bf16[1024,16,128]{2,1,0:T(8,128)(2,1)}, bf16[1024,16,128]{2,1,0:T(8,128)(2,1)}, u32[]{:S(2)}, u32[]{:S(2)}) collective-permute-start(bf16[1024,16,128]{2,1,0:T(8,128)(2,1)} %collective-permute-done.3.xa_ref), channel_id=1, source_target_pairs={{0,1},{1,0},{2,3},{3,2},{4,5},{5,4},{6,7},{7,6},{8,9},{9,8},{10,11... | collective-permute-start | bytes 12582920 | tf_op jit(solution)/shard_map/ppermute | solution.py:423
  186.4 130.7 %collective-permute-start.5 = (f32[1024,16,128]{2,1,0:T(8,128)}, f32[1024,16,128]{2,1,0:T(8,128)}, u32[]{:S(2)}, u32[]{:S(2)}) collective-permute-start(f32[1024,16,128]{2,1,0:T(8,128)} %bitcast.39), channel_id=1, source_target_pairs={{0,1},{1,0},{2,3},{3,2},{4,5},{5,4},{6,7},{7,6},{8,9},{9,8},{10,11... | collective-permute-start | bytes 25165832 | tf_op jit(solution)/shard_map/ppermute | solution.py:423
  265.8 59.6 %collective-permute-start.6 = (f32[1024,16,128]{2,1,0:T(8,128)}, f32[1024,16,128]{2,1,0:T(8,128)}, u32[]{:S(2)}, u32[]{:S(2)}) collective-permute-start(f32[1024,16,128]{2,1,0:T(8,128)} %bitcast.40), channel_id=1, source_target_pairs={{0,1},{1,0},{2,3},{3,2},{4,5},{5,4},{6,7},{7,6},{8,9},{9,8},{10,11... | collective-permute-start | bytes 25165832 | tf_op jit(solution)/shard_map/ppermute | solution.py:423
  266.2 48.1 %collective-permute-start.2 = (bf16[1024,16,128]{2,1,0:T(8,128)(2,1)}, bf16[1024,16,128]{2,1,0:T(8,128)(2,1)}, u32[]{:S(2)}, u32[]{:S(2)}) collective-permute-start(bf16[1024,16,128]{2,1,0:T(8,128)(2,1)} %bitcast.35), channel_id=1, source_target_pairs={{6,0},{3,1},{0,2},{5,3},{2,4},{7,5},{4,6},{1,7},{14,8},{11,9},{8,1... | collective-permute-start | bytes 12582920 | tf_op jit(solution)/shard_map/ppermute | solution.py:423
  314.3 19.4 %collective-permute-start.7 = (bf16[1024,16,128]{2,1,0:T(8,128)(2,1)}, bf16[1024,16,128]{2,1,0:T(8,128)(2,1)}, u32[]{:S(2)}, u32[]{:S(2)}) collective-permute-start(bf16[1024,16,128]{2,1,0:T(8,128)(2,1)} %collective-permute-done.2.xa_ref), channel_id=1, source_target_pairs={{0,1},{1,0},{2,3},{3,2},{4,5},{5,4},{6,7},{7,6},{8,9},{9,8},{10,11... | collective-permute-start | bytes 12582920 | tf_op jit(solution)/shard_map/ppermute | solution.py:423
  412.5 17.7 %collective-permute-start.8 = (f32[1024,16,128]{2,1,0:T(8,128)}, f32[1024,16,128]{2,1,0:T(8,128)}, u32[]{:S(2)}, u32[]{:S(2)}) collective-permute-start(f32[1024,16,128]{2,1,0:T(8,128)} %bitcast.38), channel_id=1, source_target_pairs={{0,1},{1,0},{2,3},{3,2},{4,5},{5,4},{6,7},{7,6},{8,9},{9,8},{10,11... | collective-permute-start | bytes 25165832 | tf_op jit(solution)/shard_map/ppermute | solution.py:423
  412.8 25.6 %collective-permute-start.9 = (bf16[1024,16,128]{2,1,0:T(8,128)(2,1)}, bf16[1024,16,128]{2,1,0:T(8,128)(2,1)}, u32[]{:S(2)}, u32[]{:S(2)}) collective-permute-start(bf16[1024,16,128]{2,1,0:T(8,128)(2,1)} %bitcast.36), channel_id=1, source_target_pairs={{0,1},{1,0},{2,3},{3,2},{4,5},{5,4},{6,7},{7,6},{8,9},{9,8},{10,11... | collective-permute-start | bytes 12582920 | tf_op jit(solution)/shard_map/ppermute | solution.py:423
  413.8 120.6 %collective-permute-start.11 = (bf16[1024,16,128]{2,1,0:T(8,128)(2,1)}, bf16[1024,16,128]{2,1,0:T(8,128)(2,1)}, u32[]{:S(2)}, u32[]{:S(2)}) collective-permute-start(bf16[1024,16,128]{2,1,0:T(8,128)(2,1)} %shard_map.104), channel_id=1, source_target_pairs={{6,0},{3,1},{0,2},{5,3},{2,4},{7,5},{4,6},{1,7},{14,8},{11,9},{8,1... | collective-permute-start | bytes 12582920 | tf_op jit(solution)/shard_map/ppermute | solution.py:423
  415.3 119.1 %collective-permute-start.12 = (bf16[1024,16,128]{2,1,0:T(8,128)(2,1)}, bf16[1024,16,128]{2,1,0:T(8,128)(2,1)}, u32[]{:S(2)}, u32[]{:S(2)}) collective-permute-start(bf16[1024,16,128]{2,1,0:T(8,128)(2,1)} %shard_map.105), channel_id=1, source_target_pairs={{0,4},{1,5},{2,6},{3,7},{4,0},{5,1},{6,2},{7,3},{8,12},{9,13},{10,... | collective-permute-start | bytes 12582920 | tf_op jit(solution)/shard_map/ppermute | solution.py:423
  516.0 18.4 %collective-permute-start.10 = (bf16[1024,16,128]{2,1,0:T(8,128)(2,1)}, bf16[1024,16,128]{2,1,0:T(8,128)(2,1)}, u32[]{:S(2)}, u32[]{:S(2)}) collective-permute-start(bf16[1024,16,128]{2,1,0:T(8,128)(2,1)} %get-tuple-element.47), channel_id=1, source_target_pairs={{0,1},{1,0},{2,3},{3,2},{4,5},{5,4},{6,7},{7,6},{8,9},{9,8},{10,11... | collective-permute-start | bytes 12582920 | tf_op jit(solution)/shard_map/ppermute | solution.py:423
  518.5 80.4 %collective-permute-start.13 = (bf16[1024,16,128]{2,1,0:T(8,128)(2,1)}, bf16[1024,16,128]{2,1,0:T(8,128)(2,1)}, u32[]{:S(2)}, u32[]{:S(2)}) collective-permute-start(bf16[1024,16,128]{2,1,0:T(8,128)(2,1)} %shard_map.108), channel_id=1, source_target_pairs={{0,6},{1,3},{2,0},{3,5},{4,2},{5,7},{6,4},{7,1},{8,14},{9,11},{10,... | collective-permute-start | bytes 12582920 | tf_op jit(solution)/shard_map/ppermute | solution.py:423

commit v3 on v2

--- a/solution.py
+++ b/solution.py
@@ -8,27 +8,30 @@
 
 ROUTE_SCALE = 16.0
 LANES = 128
-
-
-def route_tables(hidden, w_router, top_idx, keep_mask):
+SPARE = 8
+
+
+def route_tables(hidden, w_router, top_idx, keep_mask, cap):
     tokens, top_k = top_idx.shape
     experts = w_router.shape[1]
-    width, unroll = 256, 4
-
-    def kernel(x_ref, w_ref, idx_ref, keep_ref, tok_ref, gate_ref, slot_t, parts_t):
-        logits = jnp.dot(x_ref[...], w_ref[...], preferred_element_type=jnp.float32)
-        top = jnp.max(logits, axis=-1, keepdims=True)
-        ex = jnp.exp(logits - top)
-        prob = ex / jnp.sum(ex, axis=-1, keepdims=True)
+    width, unroll = cap, 4
+
+    def kernel(x_ref, w_ref, idx_ref, keep_ref, tok_ref, gate_ref, slot_t, parts_t, xv, sem):
+        load = pltpu.make_async_copy(x_ref, xv, sem)
+        load.start()
         lane = lax.broadcasted_iota(jnp.int32, (tokens, experts), 1)
         member = jnp.zeros((tokens, experts), jnp.float32)
         for k in range(top_k):
             hit = (idx_ref[:, k:k + 1] == lane) & (keep_ref[:, k:k + 1] > 0)
             member = jnp.where(hit, 1.0, member)
-        gates = ROUTE_SCALE * prob * member
         before = lax.broadcasted_iota(jnp.int32, (tokens, tokens), 0) >= lax.broadcasted_iota(jnp.int32, (tokens, tokens), 1)
         rank = jnp.dot(jnp.where(before, 1.0, 0.0).astype(jnp.bfloat16), member.astype(jnp.bfloat16), preferred_element_type=jnp.float32)
         slot = jnp.where(member > 0.0, rank - 1.0, -1.0)
+        load.wait()
+        logits = jnp.dot(xv[...], w_ref[...], preferred_element_type=jnp.float32)
+        top = jnp.max(logits, axis=-1, keepdims=True)
+        ex = jnp.exp(logits - top)
+        gates = ROUTE_SCALE * (ex / jnp.sum(ex, axis=-1, keepdims=True)) * member
         pad = jnp.zeros((tokens, LANES - experts), jnp.float32)
         slot_t[...] = jnp.transpose(jnp.concatenate([slot, pad], axis=1))[:experts]
         gt = jnp.transpose(jnp.concatenate([gates, pad], axis=1))[:experts]
@@ -43,6 +46,8 @@
         base = jnp.where(row == 0, (col // 32).astype(jnp.float32), jnp.where(row == 1, (col % 32).astype(jnp.float32), jnp.where(row == 2, 1.0, 0.0)))
         want = lax.broadcasted_iota(jnp.int32, (width, tokens), 0).astype(jnp.float32)
 
+        spare = (tokens + lax.broadcasted_iota(jnp.int32, (1, width), 1) % SPARE).astype(jnp.float32)
+
         @pl.loop(0, experts // unroll)
         def _(i):
             for u in range(unroll):
@@ -52,7 +57,7 @@
                 for q in range(3):
                     vrows = jnp.where(row == 3 + q, parts_t[q, pl.ds(e, 1), :], vrows)
                 res = lax.dot_general(vrows.astype(jnp.bfloat16), onehot, (((1,), (1,)), ((), ())), preferred_element_type=jnp.float32)
-                tok = jnp.where(res[2:3] > 0.5, res[0:1] * 32.0 + res[1:2], float(tokens))
+                tok = jnp.where(res[2:3] > 0.5, res[0:1] * 32.0 + res[1:2], spare)
                 tok_ref[pl.ds(e, 1), :] = tok
                 gate_ref[pl.ds(e, 1), :] = (res[5:6] + res[4:5]) + res[3:4]
 
@@ -60,11 +65,13 @@
     return pl.pallas_call(
         kernel,
         out_shape=[jax.ShapeDtypeStruct((experts, width), jnp.float32)] * 2,
-        in_specs=[vmem] * 4,
+        in_specs=[pl.BlockSpec(memory_space=pl.ANY)] + [vmem] * 3,
         out_specs=[vmem] * 2,
         scratch_shapes=[
             pltpu.VMEM((experts, tokens), jnp.float32),
             pltpu.VMEM((3, experts, tokens), jnp.float32),
+            pltpu.VMEM(hidden.shape, hidden.dtype),
+            pltpu.SemaphoreType.DMA,
         ],
         compiler_params=pltpu.CompilerParams(vmem_limit_bytes=48 * 1024 * 1024),
         cost_estimate=pl.CostEstimate(flops=20_000_000_000, bytes_accessed=8_000_000, transcendentals=100_000),
@@ -75,13 +82,13 @@
     return [(n * i // parts, n * (i + 1) // parts) for i in range(parts)]
 
 
-def expert_pass(ids, xa, xb, tok, gate, w1, w3, w2, cap, b_dtype, G=4):
+def expert_pass(ids, xa, xb, tok, gate, w1, w3, w2, cap, b_dtype):
     T, C, L = xa.shape
     E, D, F = w1.shape
     M = 2 * cap
     S = M + 1
     nU, nD = F // 128, D // 256
-    base = (2 * T + 2) * C
+    base = 2 * (T + SPARE) * C
     mark = -(-(base + C * S) // 8) * 8
     narrow = b_dtype == jnp.bfloat16
 
@@ -96,7 +103,7 @@
             return [pltpu.make_async_copy(src.at[e], dst.at[p], wsem.at[p, i]) for i, (src, dst) in enumerate(((w1_ref, w1v), (w3_ref, w3v), (w2_ref, w2v)))]
 
         def spread(e, b, c):
-            t = tok_ref[first[b] + e, c] + b * (T + 1)
+            t = tok_ref[first[b] + e, c] + b * (T + SPARE)
             mem[pl.ds(base + b * cap + c, C, stride=S), :] = xv[t].astype(jnp.float32)
 
         def convert(j):
@@ -105,21 +112,22 @@
         def scatter(e, b, cols):
             vals = []
             for c in cols:
-                t = tok_ref[first[b] + e, c] + b * (T + 1)
+                t = tok_ref[first[b] + e, c] + b * (T + SPARE)
                 at = pl.ds(pl.multiple_of(t * C, C), C)
                 vals.append((at, mem[at, :] + gate_ref[first[b] + e, c] * mem[pl.ds(base + b * cap + c, C, stride=S), :]))
             for at, v in vals:
                 mem[at, :] = v
 
-        loads = [pltpu.make_async_copy(x_refs[b], xv.at[pl.ds(b * (T + 1), T)], xsem.at[b]) for b in range(2)]
+        loads = [pltpu.make_async_copy(x_refs[b], xv.at[pl.ds(b * (T + SPARE), T)], xsem.at[b]) for b in range(2)]
         for c in loads: c.start()
         for c in weights(0, 0): c.start(priority=1)
         for b in range(2):
-            xv[b * (T + 1) + T] = jnp.zeros((C, L), xv.dtype)
-
-        @pl.loop(0, (2 * T + 2) // 10)
+            for k in range(SPARE):
+                xv[b * (T + SPARE) + T + k] = jnp.zeros((C, L), xv.dtype)
+
+        @pl.loop(0, 2 * (T + SPARE) // 16)
         def _(i):
-            mem[pl.ds(pl.multiple_of(i * 10 * C, 8), 10 * C), :] = jnp.zeros((10 * C, L), jnp.float32)
+            mem[pl.ds(pl.multiple_of(i * 16 * C, 8), 16 * C), :] = jnp.zeros((16 * C, L), jnp.float32)
 
         for c in lists: c.wait()
         for b in range(2):
@@ -149,8 +157,8 @@
             for k in range(2):
                 mem[pl.ds(base + (2 * n + k) * S, M), :] = h[:, L * k:L * k + L]
 
-        groups = [(b, [q + u for u in range(G)]) for b in range(2) for q in range(0, cap, G)]
-        parts = split(len(groups), nU)
+        rows_of = [(b, c) for b in range(2) for c in range(cap)]
+        parts = split(M, 2 * nU)
 
         @pl.loop(0, E)
         def _(e):
@@ -164,14 +172,11 @@
                 for c in weights(e + 1, 1 - p): c.start(priority=1)
 
             for n in range(nU):
-                for b, cols in groups[slice(*parts[n])]:
-                    scatter(prev, b, cols)
-                    for c in cols: spread(ahead, b, c)
-                if n > 0:
-                    up_tile(p, n, 0, M)
-                else:
-                    up_tile(p, n, 0, M // 2)
-                    up_tile(p, n, M // 2, M)
+                for q in range(2):
+                    for b, c in rows_of[slice(*parts[2 * n + q])]:
+                        scatter(prev, b, [c])
+                        spread(ahead, b, c)
+                    up_tile(p, n, q * M // 2, (q + 1) * M // 2)
             for n in range(nD):
                 convert(2 * n)
                 convert(2 * n + 1)
@@ -180,7 +185,7 @@
         def out(b):
             if b and narrow:
                 return pltpu.make_async_copy(xv.at[pl.ds(0, T)], ob_ref, osem.at[b])
-            return pltpu.make_async_copy(mem.at[pl.ds(b * (T + 1) * C, T * C)], (oa_ref, ob_ref)[b], osem.at[b])
+            return pltpu.make_async_copy(mem.at[pl.ds(b * (T + SPARE) * C, T * C)], (oa_ref, ob_ref)[b], osem.at[b])
 
         for b in range(2):
             @pl.loop(0, cap // 8)
@@ -192,7 +197,7 @@
                 def _(i):
                     for u in range(8):
                         r = i * 8 + u
-                        xv[r] = mem[pl.ds(pl.multiple_of((T + 1 + r) * C, C), C), :].astype(b_dtype)
+                        xv[r] = mem[pl.ds(pl.multiple_of((T + SPARE + r) * C, C), C), :].astype(b_dtype)
             out(b).start()
         for b in range(2):
             out(b).wait()
@@ -206,7 +211,7 @@
         in_specs=[smem] + [anyspec] * 7,
         out_specs=[anyspec] * 2,
         scratch_shapes=[
-            pltpu.VMEM((2 * T + 2, C, L), jnp.bfloat16),
+            pltpu.VMEM((2 * (T + SPARE), C, L), jnp.bfloat16),
             pltpu.VMEM((mark + 8, L), jnp.float32),
             pltpu.VMEM((2, D, F), jnp.bfloat16), pltpu.VMEM((2, D, F), jnp.bfloat16), pltpu.VMEM((2, F, D), jnp.bfloat16),
             pltpu.VMEM((C, M, L), jnp.bfloat16),
@@ -353,7 +358,7 @@
 
 def add_partials(pa, q):
     tokens, C, L = pa.shape
-    n, depth = 16, 6
+    n, depth = 16, 10
     rows = tokens // n
 
     def kernel(a_ref, q_ref, out_ref, av, qv, cv, asem, qsem, csem):
@@ -424,7 +429,7 @@
 
         x0 = hidden.reshape(tokens, width // LANES, LANES)
         x1 = perm(x0, near)
-        tok, gate = route_tables(after(hidden, x0), w_router, top_idx, keep_mask)
+        tok, gate = route_tables(after(hidden, x0), w_router, top_idx, keep_mask, cap)
         table = jnp.stack([tok, gate], axis=0).reshape(2, n_dev, per_dev, tok.shape[1])
         table = lax.all_to_all(table, "ep", 1, 1, tiled=False)
         table = table.reshape(2, experts, tok.shape[1])

time: 619 us -> 604 us (0.976)
  Pallas kernels: 420 us -> 400 us
    pallas_call x4, Pallas kernels: 314 us -> 295 us  [expert_pass(): pl.pallas_call(kernel, out_shape=[jax.ShapeDtypeStruct((T * C, L), jnp.fl...]
  transfers between devices with their start and end apart: 15 -> 15, of which waited for: 4 -> 4; matrix products, arithmetic and copies ran while one was open for 1% -> 1% of each run, Pallas kernels for 53% -> 52%
where the time goes in v3:
time: 604 us; the launch traced here: 598 us
  Pallas kernels  400 us (66%)
  waiting for transfers between devices  165 us (27%)
  starting transfers between devices  20.9 us (3%)
  local copies, waits for them, and re-layouts  6.54 us (1%)
    pallas_call x4, Pallas kernels, expert_pass(): pl.pallas_call(kernel, out_shape=[jax.ShapeDtypeStruct((T * C, L), jnp.fl...  295 us
    ppermute x14, waiting for transfers between devices, perm(): return lax.ppermute(v, 'ep', p)  163 us
    pallas_call x3, Pallas kernels, shared_rows(): pl.pallas_call(kernel, out_shape=jax.ShapeDtypeStruct((tokens, width), jn...  53.4 us
    pallas_call x3, Pallas kernels, add_partials(): pl.pallas_call(kernel, out_shape=jax.ShapeDtypeStruct(pa.shape, jnp.bfloa...  24.8 us
    pallas_call x1, Pallas kernels, finish(): pl.pallas_call(kernel, out_shape=jax.ShapeDtypeStruct((tokens, width), jn...  13.9 us
    ppermute x14, starting transfers between devices, perm(): return lax.ppermute(v, 'ep', p)  13.8 us
    pallas_call x1, Pallas kernels, route_tables(): pl.pallas_call(kernel, out_shape=[jax.ShapeDtypeStruct((experts, width),...  13.5 us
  transfers between devices with their start and end apart: 15, of which 4 were waited for; matrix products, arithmetic and copies ran while one was open for 1% of the time, Pallas kernels for 52%

profile of v3, /device:TPU:113, one launch (start us, length us, event | category | flops | bytes accessed | tf_op | source)
XLA Modules:
  0.0 598.4 jit_solution(4956318733669002034)
XLA Ops:
  0.0 3.6 copy.21
  3.7 1.4 collective-permute-start
  5.1 47.6 %collective-permute-done.xa_ref = bf16[1024,16,128]{2,1,0:T(8,128)(2,1)} collective-permute-done((bf16[1024,16,128]{2,1,0:T(8,128)(2,1)S(1)}, bf16[1024,16,128]{2,1,0:T(8,128)(2,1)}, u32[]{:S(2)}, u32[]{:S(2)}) %collective-permute-start) | collective-permute-done | bytes 4194336 | tf_op jit(solution)/shard_map/ppermute | solution.py:428
  52.6 0.9 collective-permute-start.1
  53.5 0.8 collective-permute-start.3
  55.1 2.2 copy-done
  57.3 13.5 %shard_map.100 = (f32[64,192]{1,0:T(8,128)S(1)}, f32[64,192]{1,0:T(8,128)S(1)}) custom-call(bf16[1024,2048]{1,0:T(8,128)(2,1)S(1)} %copy-done, bf16[2048,64]{1,0:T(8,128)(2,1)S(1)} %copy.16.w_ref, s32[1024,6]{1,0:T(8,128)S(1)} %copy.17.idx_ref, s32[1024,6]{1,0:T(8,128)S(1)} %copy.18.keep_ref), custom_call_target="tpu_custom_call" | custom-call | flops 20000000000 | bytes 8000000 | tf_op jit(solution)/shard_map/pallas_call | solution.py:65
  70.8 0.7 pad_maximum_fusion
  71.5 7.1 %all-to-all-start = ((f32[2,8,8,192]{3,2,0,1:T(8,128)}), f32[2,8,8,192]{3,2,0,1:T(8,128)}, u32[]{:S(2)}, u32[]{:S(2)}) async-start(f32[2,8,8,192]{3,2,0,1:T(8,128)} %pad_maximum_fusion), calls=%async_computation | async-start | bytes 262144 | tf_op jit(solution)/shard_map/all_to_all | solution.py:434
  78.7 0.6 pad_add_fusion.2.ids_ref
  79.3 23.6 %shard_map.101.rest_0_ = f32[1024,2048]{1,0:T(8,128)} custom-call(bf16[1024,2048]{1,0:T(8,128)(2,1)} %x_ref.3, bf16[2048,2816]{1,0:T(8,128)(2,1)} %g_ref.5, bf16[2048,2816]{1,0:T(8,128)(2,1)} %u_ref.5, bf16[2816,2048]{1,0:T(8,128)(2,1)} %d_ref.5), custom_call_target="tpu_custom_call" | custom-call | flops 17716740096 | bytes 34603008 | tf_op jit(solution)/shard_map/pallas_call | solution.py:285
  103.4 2.4 all-to-all-done
  105.9 1.5 slice_bitcast_fusion
  107.6 74.0 %shard_map.102 = (f32[16384,128]{1,0:T(8,128)}, f32[16384,128]{1,0:T(8,128)}) custom-call(s32[2]{0:T(128)} %pad_add_fusion.2.ids_ref, s32[64,192]{1,0:T(8,128)} %get-tuple-element.50.tok_all, f32[64,192]{1,0:T(8,128)} %get-tuple-element.49.gate_all, bf16[1024,16,128]{2,1,0:T(8,128)(2,1)} %collective-permute-done.xa_ref, ...), custom_call_target="tpu_custom_call" | custom-call | flops 53150220288 | bytes 138412032 | tf_op jit(solution)/shard_map/pallas_call | solution.py:208
  182.1 73.9 %shard_map.103 = (f32[16384,128]{1,0:T(8,128)}, f32[16384,128]{1,0:T(8,128)}) custom-call(s32[2]{0:T(128)} %pad_add_fusion.3.ids_ref, s32[64,192]{1,0:T(8,128)} %get-tuple-element.50.tok_all, f32[64,192]{1,0:T(8,128)} %get-tuple-element.49.gate_all, bf16[1024,16,128]{2,1,0:T(8,128)(2,1)} %collective-permute-done.3.xa_ref, ...), custom_call_target="tpu_custom_call" | custom-call | flops 53150220288 | bytes 138412032 | tf_op jit(solution)/shard_map/pallas_call | solution.py:208
  256.3 2.5 collective-permute-start.2
  258.8 45.8 %collective-permute-done.2.xa_ref = bf16[1024,16,128]{2,1,0:T(8,128)(2,1)} collective-permute-done((bf16[1024,16,128]{2,1,0:T(8,128)(2,1)}, bf16[1024,16,128]{2,1,0:T(8,128)(2,1)}, u32[]{:S(2)}, u32[]{:S(2)}) %collective-permute-start.2) | collective-permute-done | bytes 4194336 | tf_op jit(solution)/shard_map/ppermute | solution.py:428
  304.6 2.1 collective-permute-start.7
  306.6 0.7 pad_add_fusion.1.ids_ref
  307.3 8.2 %shard_map.104 = bf16[1024,16,128]{2,1,0:T(8,128)(2,1)} custom-call(f32[1024,16,128]{2,1,0:T(8,128)} %bitcast.31, f32[1024,16,128]{2,1,0:T(8,128)} %collective-permute-done.5.q_ref), custom_call_target="tpu_custom_call" | custom-call | flops 2097152 | bytes 20971520 | tf_op jit(solution)/shard_map/pallas_call | solution.py:390
  315.6 8.3 %shard_map.105 = bf16[1024,16,128]{2,1,0:T(8,128)(2,1)} custom-call(f32[1024,16,128]{2,1,0:T(8,128)} %bitcast.32, f32[1024,16,128]{2,1,0:T(8,128)} %collective-permute-done.6.q_ref), custom_call_target="tpu_custom_call" | custom-call | flops 2097152 | bytes 20971520 | tf_op jit(solution)/shard_map/pallas_call | solution.py:390
  323.8 74.0 %shard_map.106 = (f32[16384,128]{1,0:T(8,128)}, f32[16384,128]{1,0:T(8,128)}) custom-call(s32[2]{0:T(128)} %pad_add_fusion.1.ids_ref, s32[64,192]{1,0:T(8,128)} %get-tuple-element.50.tok_all, f32[64,192]{1,0:T(8,128)} %get-tuple-element.49.gate_all, bf16[1024,16,128]{2,1,0:T(8,128)(2,1)} %collective-permute-done.2.xa_ref, ...), custom_call_target="tpu_custom_call" | custom-call | flops 53150220288 | bytes 138412032 | tf_op jit(solution)/shard_map/pallas_call | solution.py:208
  398.5 0.7 pad_add_fusion.ids_ref
  399.1 1.4 collective-permute-start.11
  400.5 14.9 %shard_map.107.rest_0_ = f32[1024,2048]{1,0:T(8,128)} custom-call(bf16[1024,2048]{1,0:T(8,128)(2,1)} %x_ref.3, bf16[2048,2816]{1,0:T(8,128)(2,1)} %g_ref.5, bf16[2048,2816]{1,0:T(8,128)(2,1)} %u_ref.5, bf16[2816,2048]{1,0:T(8,128)(2,1)} %d_ref.5, f32[1024,2048]{1,0:T(8,128)} %shard_map.101.rest_0_), custom_call_target="tpu_custom_call", output_to_operand_aliasing={{}: (4, {})} | custom-call | flops 8858370048 | bytes 34603008 | tf_op jit(solution)/shard_map/pallas_call | solution.py:285
  415.4 8.3 %shard_map.108 = bf16[1024,16,128]{2,1,0:T(8,128)(2,1)} custom-call(f32[1024,16,128]{2,1,0:T(8,128)} %bitcast.30, f32[1024,16,128]{2,1,0:T(8,128)} %collective-permute-done.8.q_ref), custom_call_target="tpu_custom_call" | custom-call | flops 2097152 | bytes 20971520 | tf_op jit(solution)/shard_map/pallas_call | solution.py:390
  423.7 72.8 %shard_map.109 = (f32[16384,128]{1,0:T(8,128)}, bf16[1024,16,128]{2,1,0:T(8,128)(2,1)}) custom-call(s32[2]{0:T(128)} %pad_add_fusion.ids_ref, s32[64,192]{1,0:T(8,128)} %get-tuple-element.50.tok_all, f32[64,192]{1,0:T(8,128)} %get-tuple-element.49.gate_all, bf16[1024,16,128]{2,1,0:T(8,128)(2,1)} %bitcast.37, ...), custom_call_target="tpu_custom_call" | custom-call | flops 53150220288 | bytes 138412032 | tf_op jit(solution)/shard_map/pallas_call | solution.py:208
  496.5 2.2 collective-permute-start.10
  498.7 0.9 collective-permute-start.13
  499.7 14.9 %shard_map.110.ys_ref = f32[1024,2048]{1,0:T(8,128)} custom-call(bf16[1024,2048]{1,0:T(8,128)(2,1)} %x_ref.3, bf16[2048,2816]{1,0:T(8,128)(2,1)} %g_ref.5, bf16[2048,2816]{1,0:T(8,128)(2,1)} %u_ref.5, bf16[2816,2048]{1,0:T(8,128)(2,1)} %d_ref.5, f32[1024,2048]{1,0:T(8,128)} %shard_map.107.rest_0_), custom_call_target="tpu_custom_call", output_to_operand_aliasing={{}: (4, {})} | custom-call | flops 8858370048 | bytes 34603008 | tf_op jit(solution)/shard_map/pallas_call | solution.py:285
  514.6 69.4 %collective-permute-done.13.r3_ref = bf16[1024,16,128]{2,1,0:T(8,128)(2,1)} collective-permute-done((bf16[1024,16,128]{2,1,0:T(8,128)(2,1)}, bf16[1024,16,128]{2,1,0:T(8,128)(2,1)}, u32[]{:S(2)}, u32[]{:S(2)}) %collective-permute-start.13) | collective-permute-done | bytes 4194336 | tf_op jit(solution)/shard_map/ppermute | solution.py:428
  584.0 13.9 %shard_map.111 = bf16[1024,2048]{1,0:T(8,128)(2,1)} custom-call(f32[1024,2048]{1,0:T(8,128)} %shard_map.110.ys_ref, f32[1024,16,128]{2,1,0:T(8,128)} %bitcast.33, bf16[1024,16,128]{2,1,0:T(8,128)(2,1)} %collective-permute-done.10.q_ref, bf16[1024,16,128]{2,1,0:T(8,128)(2,1)} %collective-permute-done.11.r1_ref, ...), custom_call_target="tpu_custom_call" | custom-call | flops 12582912 | bytes 41943040 | tf_op jit(solution)/shard_map/pallas_call | solution.py:344
  (30 shorter events, 2.9 us)
Async XLA Ops:
  0.0 54.3 %copy-start.2 = (bf16[2048,64]{0,1:T(8,128)(2,1)S(1)}, bf16[2048,64]{0,1:T(8,128)(2,1)}, u32[]{:S(2)}) copy-start(bf16[2048,64]{0,1:T(8,128)(2,1)} %param.11) | copy-start | bytes 786436
  0.0 54.6 %copy-start.3 = (s32[1024,6]{0,1:T(8,128)S(1)}, s32[1024,6]{0,1:T(8,128)}, u32[]{:S(2)}) copy-start(s32[1024,6]{0,1:T(8,128)} %param.18) | copy-start | bytes 73732
  0.0 54.8 %copy-start.4 = (s32[1024,6]{0,1:T(8,128)S(1)}, s32[1024,6]{0,1:T(8,128)}, u32[]{:S(2)}) copy-start(s32[1024,6]{0,1:T(8,128)} %param.19) | copy-start | bytes 73732
  3.6 49.9 %copy-start.1 = (bf16[128,8,16,128]{3,2,1,0:T(8,128)(2,1)}, bf16[128,8,16,128]{3,2,1,0:T(8,128)(2,1)S(1)}, u32[]{:S(2)}) copy-start(bf16[128,8,16,128]{3,2,1,0:T(8,128)(2,1)S(1)} %copy.21) | copy-start | bytes 12582916
  3.7 49.0 %collective-permute-start = (bf16[1024,16,128]{2,1,0:T(8,128)(2,1)S(1)}, bf16[1024,16,128]{2,1,0:T(8,128)(2,1)}, u32[]{:S(2)}, u32[]{:S(2)}) collective-permute-start(bf16[1024,16,128]{2,1,0:T(8,128)(2,1)S(1)} %bitcast.34), channel_id=1, source_target_pairs={{0,6},{1,3},{2,0},{3,5},{4,2},{5,7},{6,4},{7,1},{8,14},{9,11},{10,... | collective-permute-start | bytes 12582920 | tf_op jit(solution)/shard_map/ppermute | solution.py:428
  52.6 54.7 %collective-permute-start.1 = (bf16[1024,16,128]{2,1,0:T(8,128)(2,1)}, bf16[1024,16,128]{2,1,0:T(8,128)(2,1)}, u32[]{:S(2)}, u32[]{:S(2)}) collective-permute-start(bf16[1024,16,128]{2,1,0:T(8,128)(2,1)} %collective-permute-done.xa_ref), channel_id=1, source_target_pairs={{0,1},{1,0},{2,3},{3,2},{4,5},{5,4},{6,7},{7,6},{8,9},{9,8},{10,11... | collective-permute-start | bytes 12582920 | tf_op jit(solution)/shard_map/ppermute | solution.py:428
  53.5 53.8 %collective-permute-start.3 = (bf16[1024,16,128]{2,1,0:T(8,128)(2,1)}, bf16[1024,16,128]{2,1,0:T(8,128)(2,1)}, u32[]{:S(2)}, u32[]{:S(2)}) collective-permute-start(bf16[1024,16,128]{2,1,0:T(8,128)(2,1)} %collective-permute-done.xa_ref), channel_id=1, source_target_pairs={{0,6},{1,3},{2,0},{3,5},{4,2},{5,7},{6,4},{7,1},{8,14},{9,11},{10,... | collective-permute-start | bytes 12582920 | tf_op jit(solution)/shard_map/ppermute | solution.py:428
  55.1 2.2 copy-start
  71.5 34.4 %all-to-all-start = ((f32[2,8,8,192]{3,2,0,1:T(8,128)}), f32[2,8,8,192]{3,2,0,1:T(8,128)}, u32[]{:S(2)}, u32[]{:S(2)}) async-start(f32[2,8,8,192]{3,2,0,1:T(8,128)} %pad_maximum_fusion), calls=%async_computation | async-start | bytes 262144 | tf_op jit(solution)/shard_map/all_to_all | solution.py:434
  107.4 74.7 %collective-permute-start.4 = (bf16[1024,16,128]{2,1,0:T(8,128)(2,1)}, bf16[1024,16,128]{2,1,0:T(8,128)(2,1)}, u32[]{:S(2)}, u32[]{:S(2)}) collective-permute-start(bf16[1024,16,128]{2,1,0:T(8,128)(2,1)} %collective-permute-done.3.xa_ref), channel_id=1, source_target_pairs={{0,1},{1,0},{2,3},{3,2},{4,5},{5,4},{6,7},{7,6},{8,9},{9,8},{10,11... | collective-permute-start | bytes 12582920 | tf_op jit(solution)/shard_map/ppermute | solution.py:428
  181.6 125.7 %collective-permute-start.5 = (f32[1024,16,128]{2,1,0:T(8,128)}, f32[1024,16,128]{2,1,0:T(8,128)}, u32[]{:S(2)}, u32[]{:S(2)}) collective-permute-start(f32[1024,16,128]{2,1,0:T(8,128)} %bitcast.39), channel_id=1, source_target_pairs={{0,1},{1,0},{2,3},{3,2},{4,5},{5,4},{6,7},{7,6},{8,9},{9,8},{10,11... | collective-permute-start | bytes 25165832 | tf_op jit(solution)/shard_map/ppermute | solution.py:428
  256.0 59.6 %collective-permute-start.6 = (f32[1024,16,128]{2,1,0:T(8,128)}, f32[1024,16,128]{2,1,0:T(8,128)}, u32[]{:S(2)}, u32[]{:S(2)}) collective-permute-start(f32[1024,16,128]{2,1,0:T(8,128)} %bitcast.40), channel_id=1, source_target_pairs={{0,1},{1,0},{2,3},{3,2},{4,5},{5,4},{6,7},{7,6},{8,9},{9,8},{10,11... | collective-permute-start | bytes 25165832 | tf_op jit(solution)/shard_map/ppermute | solution.py:428
  256.3 48.2 %collective-permute-start.2 = (bf16[1024,16,128]{2,1,0:T(8,128)(2,1)}, bf16[1024,16,128]{2,1,0:T(8,128)(2,1)}, u32[]{:S(2)}, u32[]{:S(2)}) collective-permute-start(bf16[1024,16,128]{2,1,0:T(8,128)(2,1)} %bitcast.35), channel_id=1, source_target_pairs={{6,0},{3,1},{0,2},{5,3},{2,4},{7,5},{4,6},{1,7},{14,8},{11,9},{8,1... | collective-permute-start | bytes 12582920 | tf_op jit(solution)/shard_map/ppermute | solution.py:428
  304.6 19.3 %collective-permute-start.7 = (bf16[1024,16,128]{2,1,0:T(8,128)(2,1)}, bf16[1024,16,128]{2,1,0:T(8,128)(2,1)}, u32[]{:S(2)}, u32[]{:S(2)}) collective-permute-start(bf16[1024,16,128]{2,1,0:T(8,128)(2,1)} %collective-permute-done.2.xa_ref), channel_id=1, source_target_pairs={{0,1},{1,0},{2,3},{3,2},{4,5},{5,4},{6,7},{7,6},{8,9},{9,8},{10,11... | collective-permute-start | bytes 12582920 | tf_op jit(solution)/shard_map/ppermute | solution.py:428
  397.9 17.5 %collective-permute-start.8 = (f32[1024,16,128]{2,1,0:T(8,128)}, f32[1024,16,128]{2,1,0:T(8,128)}, u32[]{:S(2)}, u32[]{:S(2)}) collective-permute-start(f32[1024,16,128]{2,1,0:T(8,128)} %bitcast.38), channel_id=1, source_target_pairs={{0,1},{1,0},{2,3},{3,2},{4,5},{5,4},{6,7},{7,6},{8,9},{9,8},{10,11... | collective-permute-start | bytes 25165832 | tf_op jit(solution)/shard_map/ppermute | solution.py:428
  398.0 25.7 %collective-permute-start.9 = (bf16[1024,16,128]{2,1,0:T(8,128)(2,1)}, bf16[1024,16,128]{2,1,0:T(8,128)(2,1)}, u32[]{:S(2)}, u32[]{:S(2)}) collective-permute-start(bf16[1024,16,128]{2,1,0:T(8,128)(2,1)} %bitcast.36), channel_id=1, source_target_pairs={{0,1},{1,0},{2,3},{3,2},{4,5},{5,4},{6,7},{7,6},{8,9},{9,8},{10,11... | collective-permute-start | bytes 12582920 | tf_op jit(solution)/shard_map/ppermute | solution.py:428
  399.1 115.5 %collective-permute-start.11 = (bf16[1024,16,128]{2,1,0:T(8,128)(2,1)}, bf16[1024,16,128]{2,1,0:T(8,128)(2,1)}, u32[]{:S(2)}, u32[]{:S(2)}) collective-permute-start(bf16[1024,16,128]{2,1,0:T(8,128)(2,1)} %shard_map.104), channel_id=1, source_target_pairs={{6,0},{3,1},{0,2},{5,3},{2,4},{7,5},{4,6},{1,7},{14,8},{11,9},{8,1... | collective-permute-start | bytes 12582920 | tf_op jit(solution)/shard_map/ppermute | solution.py:428
  400.5 114.1 %collective-permute-start.12 = (bf16[1024,16,128]{2,1,0:T(8,128)(2,1)}, bf16[1024,16,128]{2,1,0:T(8,128)(2,1)}, u32[]{:S(2)}, u32[]{:S(2)}) collective-permute-start(bf16[1024,16,128]{2,1,0:T(8,128)(2,1)} %shard_map.105), channel_id=1, source_target_pairs={{0,4},{1,5},{2,6},{3,7},{4,0},{5,1},{6,2},{7,3},{8,12},{9,13},{10,... | collective-permute-start | bytes 12582920 | tf_op jit(solution)/shard_map/ppermute | solution.py:428
  496.5 18.1 %collective-permute-start.10 = (bf16[1024,16,128]{2,1,0:T(8,128)(2,1)}, bf16[1024,16,128]{2,1,0:T(8,128)(2,1)}, u32[]{:S(2)}, u32[]{:S(2)}) collective-permute-start(bf16[1024,16,128]{2,1,0:T(8,128)(2,1)} %get-tuple-element.47), channel_id=1, source_target_pairs={{0,1},{1,0},{2,3},{3,2},{4,5},{5,4},{6,7},{7,6},{8,9},{9,8},{10,11... | collective-permute-start | bytes 12582920 | tf_op jit(solution)/shard_map/ppermute | solution.py:428
  498.7 85.3 %collective-permute-start.13 = (bf16[1024,16,128]{2,1,0:T(8,128)(2,1)}, bf16[1024,16,128]{2,1,0:T(8,128)(2,1)}, u32[]{:S(2)}, u32[]{:S(2)}) collective-permute-start(bf16[1024,16,128]{2,1,0:T(8,128)(2,1)} %shard_map.108), channel_id=1, source_target_pairs={{0,6},{1,3},{2,0},{3,5},{4,2},{5,7},{6,4},{7,1},{8,14},{9,11},{10,... | collective-permute-start | bytes 12582920 | tf_op jit(solution)/shard_map/ppermute | solution.py:428

commit v4 on v3

--- a/solution.py
+++ b/solution.py
@@ -150,12 +150,12 @@
             av[n, lo:hi] = (jax.nn.silu(h[:, :L]) * h[:, L:]).astype(jnp.bfloat16)
             mem[pl.ds(mark, 8), :] = h[:8, :L]
 
-        def down_tile(p, n):
-            act = jnp.concatenate([av[j] for j in range(nU)], axis=1)
+        def down_tile(p, n, lo, hi):
+            act = jnp.concatenate([av[j, lo:hi] for j in range(nU)], axis=1)
             h = jnp.dot(act, w2v[p, :, pl.ds(n * 256, 256)], preferred_element_type=jnp.float32)
             h = h.astype(jnp.bfloat16).astype(jnp.float32)
             for k in range(2):
-                mem[pl.ds(base + (2 * n + k) * S, M), :] = h[:, L * k:L * k + L]
+                mem[pl.ds(base + (2 * n + k) * S + lo, hi - lo), :] = h[:, L * k:L * k + L]
 
         rows_of = [(b, c) for b in range(2) for c in range(cap)]
         parts = split(M, 2 * nU)
@@ -180,7 +180,8 @@
             for n in range(nD):
                 convert(2 * n)
                 convert(2 * n + 1)
-                down_tile(p, n)
+                down_tile(p, n, 0, M // 2)
+                down_tile(p, n, M // 2, M)
 
         def out(b):
             if b and narrow:
@@ -229,7 +230,8 @@
     ff = gate_w.shape[1]
     tile = 256
     n_up, n_down = ff // tile, width // tile
-    up_parts, down_parts = split(n_up, 4), split(n_down, 2)
+    up_parts, down_parts = (split(n_up, 6), split(n_down, 4)) if 4 * rows <= tokens else (split(n_up, 4), split(n_down, 2))
+    ahead = 3 if 4 * rows <= tokens else 2
 
     def kernel(x_ref, g_ref, u_ref, d_ref, *rest):
         out_ref, xv, gv, uv, dv, act, yv, sem, usem, dsem, osem = rest[-11:]
@@ -254,11 +256,12 @@
         def arrive(i):
             for c in chunks[i]:
                 c.wait()
-            begin(i + 2)
+            begin(i + ahead)
 
         begin(0)
         load_x.wait()
-        begin(1)
+        for i in range(1, ahead):
+            begin(i)
         for i, (lo, hi) in enumerate(up_parts):
             arrive(i)
             for n in range(lo, hi):

time: 604 us -> 603 us (level)
  no operation moved by 1% of the time
where the time goes in v4:
time: 603 us; the launch traced here: 597 us
  Pallas kernels  399 us (66%)
  waiting for transfers between devices  165 us (27%)
  starting transfers between devices  20.9 us (3%)
  local copies, waits for them, and re-layouts  6.54 us (1%)
    pallas_call x4, Pallas kernels, expert_pass(): pl.pallas_call(kernel, out_shape=[jax.ShapeDtypeStruct((T * C, L), jnp.fl...  293 us
    ppermute x14, waiting for transfers between devices, perm(): return lax.ppermute(v, 'ep', p)  163 us
    pallas_call x3, Pallas kernels, shared_rows(): pl.pallas_call(kernel, out_shape=jax.ShapeDtypeStruct((tokens, width), jn...  53.5 us
    pallas_call x3, Pallas kernels, add_partials(): pl.pallas_call(kernel, out_shape=jax.ShapeDtypeStruct(pa.shape, jnp.bfloa...  24.8 us
    pallas_call x1, Pallas kernels, finish(): pl.pallas_call(kernel, out_shape=jax.ShapeDtypeStruct((tokens, width), jn...  13.9 us
    ppermute x14, starting transfers between devices, perm(): return lax.ppermute(v, 'ep', p)  13.8 us
    pallas_call x1, Pallas kernels, route_tables(): pl.pallas_call(kernel, out_shape=[jax.ShapeDtypeStruct((experts, width),...  13.5 us
  transfers between devices with their start and end apart: 15, of which 4 were waited for; matrix products, arithmetic and copies ran while one was open for 1% of the time, Pallas kernels for 52%

profile of v4, /device:TPU:113, one launch (start us, length us, event | category | flops | bytes accessed | tf_op | source)
XLA Modules:
  0.0 597.2 jit_solution(5406605890460974602)
XLA Ops:
  0.0 3.6 copy.21
  3.7 1.4 collective-permute-start
  5.1 47.6 %collective-permute-done.xa_ref = bf16[1024,16,128]{2,1,0:T(8,128)(2,1)} collective-permute-done((bf16[1024,16,128]{2,1,0:T(8,128)(2,1)S(1)}, bf16[1024,16,128]{2,1,0:T(8,128)(2,1)}, u32[]{:S(2)}, u32[]{:S(2)}) %collective-permute-start) | collective-permute-done | bytes 4194336 | tf_op jit(solution)/shard_map/ppermute | solution.py:431
  52.6 0.9 collective-permute-start.1
  53.5 0.8 collective-permute-start.3
  55.1 2.2 copy-done
  57.3 13.5 %shard_map.100 = (f32[64,192]{1,0:T(8,128)S(1)}, f32[64,192]{1,0:T(8,128)S(1)}) custom-call(bf16[1024,2048]{1,0:T(8,128)(2,1)S(1)} %copy-done, bf16[2048,64]{1,0:T(8,128)(2,1)S(1)} %copy.16.w_ref, s32[1024,6]{1,0:T(8,128)S(1)} %copy.17.idx_ref, s32[1024,6]{1,0:T(8,128)S(1)} %copy.18.keep_ref), custom_call_target="tpu_custom_call" | custom-call | flops 20000000000 | bytes 8000000 | tf_op jit(solution)/shard_map/pallas_call | solution.py:65
  70.8 0.7 pad_maximum_fusion
  71.5 7.1 %all-to-all-start = ((f32[2,8,8,192]{3,2,0,1:T(8,128)}), f32[2,8,8,192]{3,2,0,1:T(8,128)}, u32[]{:S(2)}, u32[]{:S(2)}) async-start(f32[2,8,8,192]{3,2,0,1:T(8,128)} %pad_maximum_fusion), calls=%async_computation | async-start | bytes 262144 | tf_op jit(solution)/shard_map/all_to_all | solution.py:437
  78.7 0.6 pad_add_fusion.2.ids_ref
  79.3 23.6 %shard_map.101.rest_0_ = f32[1024,2048]{1,0:T(8,128)} custom-call(bf16[1024,2048]{1,0:T(8,128)(2,1)} %x_ref.3, bf16[2048,2816]{1,0:T(8,128)(2,1)} %g_ref.5, bf16[2048,2816]{1,0:T(8,128)(2,1)} %u_ref.5, bf16[2816,2048]{1,0:T(8,128)(2,1)} %d_ref.5), custom_call_target="tpu_custom_call" | custom-call | flops 17716740096 | bytes 34603008 | tf_op jit(solution)/shard_map/pallas_call | solution.py:288
  103.4 2.4 all-to-all-done
  105.9 1.5 slice_bitcast_fusion
  107.6 73.6 %shard_map.102 = (f32[16384,128]{1,0:T(8,128)}, f32[16384,128]{1,0:T(8,128)}) custom-call(s32[2]{0:T(128)} %pad_add_fusion.2.ids_ref, s32[64,192]{1,0:T(8,128)} %get-tuple-element.50.tok_all, f32[64,192]{1,0:T(8,128)} %get-tuple-element.49.gate_all, bf16[1024,16,128]{2,1,0:T(8,128)(2,1)} %collective-permute-done.xa_ref, ...), custom_call_target="tpu_custom_call" | custom-call | flops 53150220288 | bytes 138412032 | tf_op jit(solution)/shard_map/pallas_call | solution.py:209
  181.7 73.5 %shard_map.103 = (f32[16384,128]{1,0:T(8,128)}, f32[16384,128]{1,0:T(8,128)}) custom-call(s32[2]{0:T(128)} %pad_add_fusion.3.ids_ref, s32[64,192]{1,0:T(8,128)} %get-tuple-element.50.tok_all, f32[64,192]{1,0:T(8,128)} %get-tuple-element.49.gate_all, bf16[1024,16,128]{2,1,0:T(8,128)(2,1)} %collective-permute-done.3.xa_ref, ...), custom_call_target="tpu_custom_call" | custom-call | flops 53150220288 | bytes 138412032 | tf_op jit(solution)/shard_map/pallas_call | solution.py:209
  255.6 2.4 collective-permute-start.2
  258.0 45.8 %collective-permute-done.2.xa_ref = bf16[1024,16,128]{2,1,0:T(8,128)(2,1)} collective-permute-done((bf16[1024,16,128]{2,1,0:T(8,128)(2,1)}, bf16[1024,16,128]{2,1,0:T(8,128)(2,1)}, u32[]{:S(2)}, u32[]{:S(2)}) %collective-permute-start.2) | collective-permute-done | bytes 4194336 | tf_op jit(solution)/shard_map/ppermute | solution.py:431
  303.8 2.1 collective-permute-start.7
  305.9 0.7 pad_add_fusion.1.ids_ref
  306.5 8.2 %shard_map.104 = bf16[1024,16,128]{2,1,0:T(8,128)(2,1)} custom-call(f32[1024,16,128]{2,1,0:T(8,128)} %bitcast.31, f32[1024,16,128]{2,1,0:T(8,128)} %collective-permute-done.5.q_ref), custom_call_target="tpu_custom_call" | custom-call | flops 2097152 | bytes 20971520 | tf_op jit(solution)/shard_map/pallas_call | solution.py:393
  314.8 8.3 %shard_map.105 = bf16[1024,16,128]{2,1,0:T(8,128)(2,1)} custom-call(f32[1024,16,128]{2,1,0:T(8,128)} %bitcast.32, f32[1024,16,128]{2,1,0:T(8,128)} %collective-permute-done.6.q_ref), custom_call_target="tpu_custom_call" | custom-call | flops 2097152 | bytes 20971520 | tf_op jit(solution)/shard_map/pallas_call | solution.py:393
  323.1 73.6 %shard_map.106 = (f32[16384,128]{1,0:T(8,128)}, f32[16384,128]{1,0:T(8,128)}) custom-call(s32[2]{0:T(128)} %pad_add_fusion.1.ids_ref, s32[64,192]{1,0:T(8,128)} %get-tuple-element.50.tok_all, f32[64,192]{1,0:T(8,128)} %get-tuple-element.49.gate_all, bf16[1024,16,128]{2,1,0:T(8,128)(2,1)} %collective-permute-done.2.xa_ref, ...), custom_call_target="tpu_custom_call" | custom-call | flops 53150220288 | bytes 138412032 | tf_op jit(solution)/shard_map/pallas_call | solution.py:209
  397.3 0.7 pad_add_fusion.ids_ref
  398.0 1.4 collective-permute-start.11
  399.3 14.9 %shard_map.107.rest_0_ = f32[1024,2048]{1,0:T(8,128)} custom-call(bf16[1024,2048]{1,0:T(8,128)(2,1)} %x_ref.3, bf16[2048,2816]{1,0:T(8,128)(2,1)} %g_ref.5, bf16[2048,2816]{1,0:T(8,128)(2,1)} %u_ref.5, bf16[2816,2048]{1,0:T(8,128)(2,1)} %d_ref.5, f32[1024,2048]{1,0:T(8,128)} %shard_map.101.rest_0_), custom_call_target="tpu_custom_call", output_to_operand_aliasing={{}: (4, {})} | custom-call | flops 8858370048 | bytes 34603008 | tf_op jit(solution)/shard_map/pallas_call | solution.py:288
  414.3 8.3 %shard_map.108 = bf16[1024,16,128]{2,1,0:T(8,128)(2,1)} custom-call(f32[1024,16,128]{2,1,0:T(8,128)} %bitcast.30, f32[1024,16,128]{2,1,0:T(8,128)} %collective-permute-done.8.q_ref), custom_call_target="tpu_custom_call" | custom-call | flops 2097152 | bytes 20971520 | tf_op jit(solution)/shard_map/pallas_call | solution.py:393
  422.6 72.5 %shard_map.109 = (f32[16384,128]{1,0:T(8,128)}, bf16[1024,16,128]{2,1,0:T(8,128)(2,1)}) custom-call(s32[2]{0:T(128)} %pad_add_fusion.ids_ref, s32[64,192]{1,0:T(8,128)} %get-tuple-element.50.tok_all, f32[64,192]{1,0:T(8,128)} %get-tuple-element.49.gate_all, bf16[1024,16,128]{2,1,0:T(8,128)(2,1)} %bitcast.37, ...), custom_call_target="tpu_custom_call" | custom-call | flops 53150220288 | bytes 138412032 | tf_op jit(solution)/shard_map/pallas_call | solution.py:209
  495.0 2.2 collective-permute-start.10
  497.2 1.0 collective-permute-start.13
  498.2 15.0 %shard_map.110.ys_ref = f32[1024,2048]{1,0:T(8,128)} custom-call(bf16[1024,2048]{1,0:T(8,128)(2,1)} %x_ref.3, bf16[2048,2816]{1,0:T(8,128)(2,1)} %g_ref.5, bf16[2048,2816]{1,0:T(8,128)(2,1)} %u_ref.5, bf16[2816,2048]{1,0:T(8,128)(2,1)} %d_ref.5, f32[1024,2048]{1,0:T(8,128)} %shard_map.107.rest_0_), custom_call_target="tpu_custom_call", output_to_operand_aliasing={{}: (4, {})} | custom-call | flops 8858370048 | bytes 34603008 | tf_op jit(solution)/shard_map/pallas_call | solution.py:288
  513.2 69.6 %collective-permute-done.13.r3_ref = bf16[1024,16,128]{2,1,0:T(8,128)(2,1)} collective-permute-done((bf16[1024,16,128]{2,1,0:T(8,128)(2,1)}, bf16[1024,16,128]{2,1,0:T(8,128)(2,1)}, u32[]{:S(2)}, u32[]{:S(2)}) %collective-permute-start.13) | collective-permute-done | bytes 4194336 | tf_op jit(solution)/shard_map/ppermute | solution.py:431
  582.8 13.9 %shard_map.111 = bf16[1024,2048]{1,0:T(8,128)(2,1)} custom-call(f32[1024,2048]{1,0:T(8,128)} %shard_map.110.ys_ref, f32[1024,16,128]{2,1,0:T(8,128)} %bitcast.33, bf16[1024,16,128]{2,1,0:T(8,128)(2,1)} %collective-permute-done.10.q_ref, bf16[1024,16,128]{2,1,0:T(8,128)(2,1)} %collective-permute-done.11.r1_ref, ...), custom_call_target="tpu_custom_call" | custom-call | flops 12582912 | bytes 41943040 | tf_op jit(solution)/shard_map/pallas_call | solution.py:347
  (30 shorter events, 3.0 us)
Async XLA Ops:
  0.0 54.3 %copy-start.2 = (bf16[2048,64]{0,1:T(8,128)(2,1)S(1)}, bf16[2048,64]{0,1:T(8,128)(2,1)}, u32[]{:S(2)}) copy-start(bf16[2048,64]{0,1:T(8,128)(2,1)} %param.11) | copy-start | bytes 786436
  0.0 54.6 %copy-start.3 = (s32[1024,6]{0,1:T(8,128)S(1)}, s32[1024,6]{0,1:T(8,128)}, u32[]{:S(2)}) copy-start(s32[1024,6]{0,1:T(8,128)} %param.18) | copy-start | bytes 73732
  0.0 54.8 %copy-start.4 = (s32[1024,6]{0,1:T(8,128)S(1)}, s32[1024,6]{0,1:T(8,128)}, u32[]{:S(2)}) copy-start(s32[1024,6]{0,1:T(8,128)} %param.19) | copy-start | bytes 73732
  3.6 49.9 %copy-start.1 = (bf16[128,8,16,128]{3,2,1,0:T(8,128)(2,1)}, bf16[128,8,16,128]{3,2,1,0:T(8,128)(2,1)S(1)}, u32[]{:S(2)}) copy-start(bf16[128,8,16,128]{3,2,1,0:T(8,128)(2,1)S(1)} %copy.21) | copy-start | bytes 12582916
  3.7 49.0 %collective-permute-start = (bf16[1024,16,128]{2,1,0:T(8,128)(2,1)S(1)}, bf16[1024,16,128]{2,1,0:T(8,128)(2,1)}, u32[]{:S(2)}, u32[]{:S(2)}) collective-permute-start(bf16[1024,16,128]{2,1,0:T(8,128)(2,1)S(1)} %bitcast.34), channel_id=1, source_target_pairs={{0,6},{1,3},{2,0},{3,5},{4,2},{5,7},{6,4},{7,1},{8,14},{9,11},{10,... | collective-permute-start | bytes 12582920 | tf_op jit(solution)/shard_map/ppermute | solution.py:431
  52.6 54.7 %collective-permute-start.1 = (bf16[1024,16,128]{2,1,0:T(8,128)(2,1)}, bf16[1024,16,128]{2,1,0:T(8,128)(2,1)}, u32[]{:S(2)}, u32[]{:S(2)}) collective-permute-start(bf16[1024,16,128]{2,1,0:T(8,128)(2,1)} %collective-permute-done.xa_ref), channel_id=1, source_target_pairs={{0,1},{1,0},{2,3},{3,2},{4,5},{5,4},{6,7},{7,6},{8,9},{9,8},{10,11... | collective-permute-start | bytes 12582920 | tf_op jit(solution)/shard_map/ppermute | solution.py:431
  53.5 53.8 %collective-permute-start.3 = (bf16[1024,16,128]{2,1,0:T(8,128)(2,1)}, bf16[1024,16,128]{2,1,0:T(8,128)(2,1)}, u32[]{:S(2)}, u32[]{:S(2)}) collective-permute-start(bf16[1024,16,128]{2,1,0:T(8,128)(2,1)} %collective-permute-done.xa_ref), channel_id=1, source_target_pairs={{0,6},{1,3},{2,0},{3,5},{4,2},{5,7},{6,4},{7,1},{8,14},{9,11},{10,... | collective-permute-start | bytes 12582920 | tf_op jit(solution)/shard_map/ppermute | solution.py:431
  55.1 2.2 copy-start
  71.5 34.4 %all-to-all-start = ((f32[2,8,8,192]{3,2,0,1:T(8,128)}), f32[2,8,8,192]{3,2,0,1:T(8,128)}, u32[]{:S(2)}, u32[]{:S(2)}) async-start(f32[2,8,8,192]{3,2,0,1:T(8,128)} %pad_maximum_fusion), calls=%async_computation | async-start | bytes 262144 | tf_op jit(solution)/shard_map/all_to_all | solution.py:437
  107.4 74.3 %collective-permute-start.4 = (bf16[1024,16,128]{2,1,0:T(8,128)(2,1)}, bf16[1024,16,128]{2,1,0:T(8,128)(2,1)}, u32[]{:S(2)}, u32[]{:S(2)}) collective-permute-start(bf16[1024,16,128]{2,1,0:T(8,128)(2,1)} %collective-permute-done.3.xa_ref), channel_id=1, source_target_pairs={{0,1},{1,0},{2,3},{3,2},{4,5},{5,4},{6,7},{7,6},{8,9},{9,8},{10,11... | collective-permute-start | bytes 12582920 | tf_op jit(solution)/shard_map/ppermute | solution.py:431
  181.3 125.3 %collective-permute-start.5 = (f32[1024,16,128]{2,1,0:T(8,128)}, f32[1024,16,128]{2,1,0:T(8,128)}, u32[]{:S(2)}, u32[]{:S(2)}) collective-permute-start(f32[1024,16,128]{2,1,0:T(8,128)} %bitcast.39), channel_id=1, source_target_pairs={{0,1},{1,0},{2,3},{3,2},{4,5},{5,4},{6,7},{7,6},{8,9},{9,8},{10,11... | collective-permute-start | bytes 25165832 | tf_op jit(solution)/shard_map/ppermute | solution.py:431
  255.2 59.6 %collective-permute-start.6 = (f32[1024,16,128]{2,1,0:T(8,128)}, f32[1024,16,128]{2,1,0:T(8,128)}, u32[]{:S(2)}, u32[]{:S(2)}) collective-permute-start(f32[1024,16,128]{2,1,0:T(8,128)} %bitcast.40), channel_id=1, source_target_pairs={{0,1},{1,0},{2,3},{3,2},{4,5},{5,4},{6,7},{7,6},{8,9},{9,8},{10,11... | collective-permute-start | bytes 25165832 | tf_op jit(solution)/shard_map/ppermute | solution.py:431
  255.6 48.2 %collective-permute-start.2 = (bf16[1024,16,128]{2,1,0:T(8,128)(2,1)}, bf16[1024,16,128]{2,1,0:T(8,128)(2,1)}, u32[]{:S(2)}, u32[]{:S(2)}) collective-permute-start(bf16[1024,16,128]{2,1,0:T(8,128)(2,1)} %bitcast.35), channel_id=1, source_target_pairs={{6,0},{3,1},{0,2},{5,3},{2,4},{7,5},{4,6},{1,7},{14,8},{11,9},{8,1... | collective-permute-start | bytes 12582920 | tf_op jit(solution)/shard_map/ppermute | solution.py:431
  303.8 19.3 %collective-permute-start.7 = (bf16[1024,16,128]{2,1,0:T(8,128)(2,1)}, bf16[1024,16,128]{2,1,0:T(8,128)(2,1)}, u32[]{:S(2)}, u32[]{:S(2)}) collective-permute-start(bf16[1024,16,128]{2,1,0:T(8,128)(2,1)} %collective-permute-done.2.xa_ref), channel_id=1, source_target_pairs={{0,1},{1,0},{2,3},{3,2},{4,5},{5,4},{6,7},{7,6},{8,9},{9,8},{10,11... | collective-permute-start | bytes 12582920 | tf_op jit(solution)/shard_map/ppermute | solution.py:431
  396.7 17.6 %collective-permute-start.8 = (f32[1024,16,128]{2,1,0:T(8,128)}, f32[1024,16,128]{2,1,0:T(8,128)}, u32[]{:S(2)}, u32[]{:S(2)}) collective-permute-start(f32[1024,16,128]{2,1,0:T(8,128)} %bitcast.38), channel_id=1, source_target_pairs={{0,1},{1,0},{2,3},{3,2},{4,5},{5,4},{6,7},{7,6},{8,9},{9,8},{10,11... | collective-permute-start | bytes 25165832 | tf_op jit(solution)/shard_map/ppermute | solution.py:431
  396.8 25.7 %collective-permute-start.9 = (bf16[1024,16,128]{2,1,0:T(8,128)(2,1)}, bf16[1024,16,128]{2,1,0:T(8,128)(2,1)}, u32[]{:S(2)}, u32[]{:S(2)}) collective-permute-start(bf16[1024,16,128]{2,1,0:T(8,128)(2,1)} %bitcast.36), channel_id=1, source_target_pairs={{0,1},{1,0},{2,3},{3,2},{4,5},{5,4},{6,7},{7,6},{8,9},{9,8},{10,11... | collective-permute-start | bytes 12582920 | tf_op jit(solution)/shard_map/ppermute | solution.py:431
  398.0 115.2 %collective-permute-start.11 = (bf16[1024,16,128]{2,1,0:T(8,128)(2,1)}, bf16[1024,16,128]{2,1,0:T(8,128)(2,1)}, u32[]{:S(2)}, u32[]{:S(2)}) collective-permute-start(bf16[1024,16,128]{2,1,0:T(8,128)(2,1)} %shard_map.104), channel_id=1, source_target_pairs={{6,0},{3,1},{0,2},{5,3},{2,4},{7,5},{4,6},{1,7},{14,8},{11,9},{8,1... | collective-permute-start | bytes 12582920 | tf_op jit(solution)/shard_map/ppermute | solution.py:431
  399.3 113.9 %collective-permute-start.12 = (bf16[1024,16,128]{2,1,0:T(8,128)(2,1)}, bf16[1024,16,128]{2,1,0:T(8,128)(2,1)}, u32[]{:S(2)}, u32[]{:S(2)}) collective-permute-start(bf16[1024,16,128]{2,1,0:T(8,128)(2,1)} %shard_map.105), channel_id=1, source_target_pairs={{0,4},{1,5},{2,6},{3,7},{4,0},{5,1},{6,2},{7,3},{8,12},{9,13},{10,... | collective-permute-start | bytes 12582920 | tf_op jit(solution)/shard_map/ppermute | solution.py:431
  495.0 18.2 %collective-permute-start.10 = (bf16[1024,16,128]{2,1,0:T(8,128)(2,1)}, bf16[1024,16,128]{2,1,0:T(8,128)(2,1)}, u32[]{:S(2)}, u32[]{:S(2)}) collective-permute-start(bf16[1024,16,128]{2,1,0:T(8,128)(2,1)} %get-tuple-element.47), channel_id=1, source_target_pairs={{0,1},{1,0},{2,3},{3,2},{4,5},{5,4},{6,7},{7,6},{8,9},{9,8},{10,11... | collective-permute-start | bytes 12582920 | tf_op jit(solution)/shard_map/ppermute | solution.py:431
  497.2 85.6 %collective-permute-start.13 = (bf16[1024,16,128]{2,1,0:T(8,128)(2,1)}, bf16[1024,16,128]{2,1,0:T(8,128)(2,1)}, u32[]{:S(2)}, u32[]{:S(2)}) collective-permute-start(bf16[1024,16,128]{2,1,0:T(8,128)(2,1)} %shard_map.108), channel_id=1, source_target_pairs={{0,6},{1,3},{2,0},{3,5},{4,2},{5,7},{6,4},{7,1},{8,14},{9,11},{10,... | collective-permute-start | bytes 12582920 | tf_op jit(solution)/shard_map/ppermute | solution.py:431
